TPU v7x, 1024 devices: a whole 4x4x32 slice. The times are simulated.
1024 devices in a mesh: seq: 16 (over y, x), rep: 64 (over z, core).
Axes of the slice: x: 4, y: 4, z: 32, core: 2. Of those that a mesh axis runs over, the one named last changes fastest.
Arguments:
- mixer_in: bfloat16 [64, 2048, 4096], P('rep', 'seq'), may hold values from -6 to 6
- write_proj: bfloat16 [64, 2048, 512], P('rep', 'seq'), may hold values from -6 to 6
- read_proj: bfloat16 [64, 2048, 512], P('rep', 'seq'), may hold values from -0.5 to 0.5
- dt_steps: int32 [64, 2048, 64], P('rep', 'seq'), may hold values from 1 to 16
- decay_exp: int32 [64, 2048, 64], P('rep', 'seq'), may hold values from 1 to 50000, as said below
- norm_gain: float32 [4096], P('seq'), may hold values from 0.1 to 1.9
- skip_gain: float32 [64], P('seq'), may hold values from 1 to 4
- out_grad: bfloat16 [64, 2048, 4096], P('rep', 'seq'), may hold values from -80 to 80
Outputs:
- mixer_grad: bfloat16 [64, 2048, 4096], P('rep', 'seq')
- read_grad: bfloat16 [64, 2048, 512], P('rep', 'seq')
- gain_grad: float32 [4096], P('seq')
- skip_grad: float32 [64], P('seq')
Inputs may be any that keep to these rules, and one draw needn't show every extreme that they name: The decay factor of head h at position t is exp(-decay_exp / 65536).
All inputs are finite; a program needn't handle non-finite values.
Results may differ from a plain program's by a relative error of at most 0.015.
Values may be sent and summed in bfloat16 or wider, within the bound.
No kernel may reach another device: no remote copies, remote signals or barrier semaphores. Data moves between devices by JAX's collectives and lax.ppermute only.
A program may use at most 64 MiB of HBM per device.

v0:
```python
import functools

import jax
import jax.numpy as jnp
from jax import lax
from jax.sharding import Mesh
from jax.sharding import PartitionSpec as P

H = 64
P_SIZE = 64
N = 128
G = 4
HG = 16
SEQ = ("seq_0", "seq_1")
REP = ("rep_0", "rep_1")


def neutral_like(array, identity):
    return jax.tree.map(
        lambda a, e: jnp.broadcast_to(jnp.asarray(e, a.dtype), a.shape), array, identity
    )


def carried_in(array, axes, combine, identity, reverse):
    before = start = neutral_like(array, identity)
    total = array
    for axis in reversed(axes):
        devices, here = (lax.axis_size(axis), lax.axis_index(axis))
        pieces = jax.tree.map(lambda part: lax.all_gather(part, axis), total)
        inside, total = (start, start)
        for k in reversed(range(devices)) if reverse else range(devices):
            passed = k > here if reverse else k < here
            total = combine(total, jax.tree.map(lambda part: part[k], pieces))
            inside = jax.tree.map(lambda new, old: jnp.where(passed, new, old), total, inside)
        before = combine(inside, before)
    return before


def laid_out(blocks, dim):
    shape = list(blocks.shape[1:])
    shape[dim] *= blocks.shape[0]
    return jnp.moveaxis(blocks, 0, dim).reshape(shape)


def gather_together(arrays, axis, dims):
    line = jnp.concatenate([a.reshape(-1) for a in arrays])
    lines, at, finished = (lax.all_gather(line, axis), 0, [])
    for a, dim in zip(arrays, dims):
        blocks = lines[:, at : at + a.size].reshape(-1, *a.shape)
        finished.append(laid_out(blocks, dim))
        at += a.size
    return tuple(finished)


def in_blocks(array, dim, devices):
    shape = array.shape
    blocks = array.reshape(*shape[:dim], devices, shape[dim] // devices, *shape[dim + 1 :])
    return jnp.moveaxis(blocks, dim, 0)


def summed_on_arrival(array, axis, dim):
    blocks = in_blocks(array, dim, lax.axis_size(axis))
    arrived = lax.all_to_all(blocks, axis, split_axis=0, concat_axis=0, tiled=True)
    return arrived.sum(axis=0)


def one_axis_at_a_time(array, axes):
    return functools.reduce(lax.psum, axes, array)


def contract(form, left, right):
    return jnp.einsum(form, left, right, preferred_element_type=jnp.float32)


def decay_weights(log_decay, step_size):
    length = log_decay.shape[2]
    causal = jnp.arange(length)[:, None] >= jnp.arange(length)[None, :]
    spread = jnp.where(causal, log_decay[:, :, :, None] - log_decay[:, :, None, :], 0.0)
    return jnp.where(causal, jnp.exp(spread), 0.0) * step_size[:, :, None, :]


def block_front(mixed, write, read, steps, decay):
    length = mixed.shape[3]
    log_decay = -(
        jnp.cumsum(jnp.transpose(decay).reshape(G, HG, length), axis=2).astype(jnp.float32)
        / 65536.0
    )
    step_size = jnp.transpose(steps).reshape(G, HG, length).astype(jnp.float32) / 16.0
    weights = decay_weights(log_decay, step_size)
    scores = contract("gnt,gns->gts", read, write)
    mixing = (scores[:, None] * weights).astype(jnp.bfloat16)
    inner_part = contract("gjts,gjps->gjpt", mixing, mixed)
    ending = jnp.exp(log_decay[:, :, -1:] - log_decay) * step_size
    weighted = (mixed.astype(jnp.float32) * ending[:, :, None, :]).astype(jnp.bfloat16)
    span_state = contract("gjps,gns->gjpn", weighted, write).astype(jnp.bfloat16)
    block_decay = jnp.exp(log_decay[:, :, -1]).astype(jnp.bfloat16)
    readout = jnp.exp(log_decay)
    return (log_decay, step_size, mixing, inner_part, ending, span_state, block_decay, readout)


def block_middle(mixed, read, skip_full, gain_full, upstream, inner_part, readout, carried):
    mixed_wide = mixed.astype(jnp.float32)
    mixer_out = (
        inner_part
        + readout[:, :, None, :] * contract("gnt,gjpn->gjpt", read, carried)
        + skip_full[:, :, None, None] * mixed_wide
    )
    inverse = lax.rsqrt(jnp.mean(mixer_out * mixer_out, axis=(1, 2), keepdims=True) + 1e-05)
    normed = mixer_out * inverse
    upstream_wide = upstream.astype(jnp.float32)
    normed_grad = upstream_wide * gain_full[:, :, :, None]
    gain_part = jnp.sum(upstream_wide * normed, axis=3)
    delta_wide = inverse * (
        normed_grad - normed * jnp.mean(normed_grad * normed, axis=(1, 2), keepdims=True)
    )
    skip_part = jnp.sum(delta_wide * mixed_wide, axis=(2, 3))
    delta_half = delta_wide.astype(jnp.bfloat16)
    scaled_delta = (delta_wide * readout[:, :, None, :]).astype(jnp.bfloat16)
    state_grad = contract("gjpt,gnt->gjpn", scaled_delta, read).astype(jnp.bfloat16)
    read_part = contract("gjpt,gjpn->gnt", scaled_delta, carried)
    return (delta_wide, delta_half, state_grad, read_part, gain_part, skip_part)


def block_back(
    mixed,
    write,
    skip_full,
    log_decay,
    step_size,
    mixing,
    ending,
    delta_wide,
    delta_half,
    read_part,
    carried_grad,
):
    weights = decay_weights(log_decay, step_size)
    mix_grad = contract("gjpt,gjps->gjts", delta_half, mixed)
    score_grad = jnp.sum(mix_grad * weights, axis=1).astype(jnp.bfloat16)
    read_grad = contract("gts,gns->gnt", score_grad, write) + read_part
    mixer_grad = contract("gjts,gjpt->gjps", mixing, delta_half)
    mixer_grad = mixer_grad + ending[:, :, None, :] * contract(
        "gns,gjpn->gjps", write, carried_grad
    )
    mixer_grad = mixer_grad + skip_full[:, :, None, None] * delta_wide
    return (mixer_grad.astype(jnp.bfloat16), read_grad.astype(jnp.bfloat16))


def forward_join(earlier, later):
    decay_early, state_early = earlier
    decay_late, state_late = later
    joined = (decay_early.astype(jnp.float32) * decay_late.astype(jnp.float32)).astype(jnp.bfloat16)
    state = (
        decay_late.astype(jnp.float32)[..., None, None] * state_early.astype(jnp.float32)
        + state_late.astype(jnp.float32)
    ).astype(jnp.bfloat16)
    return (joined, state)


def backward_join(earlier, later):
    decay_early, grad_early = earlier
    decay_late, grad_late = later
    joined = (decay_early.astype(jnp.float32) * decay_late.astype(jnp.float32)).astype(jnp.bfloat16)
    grads = (
        grad_late.astype(jnp.float32)
        + decay_late.astype(jnp.float32)[..., None, None] * grad_early.astype(jnp.float32)
    ).astype(jnp.bfloat16)
    return (joined, grads)


def neutral(block_decay, span_state):
    return (jnp.ones(block_decay.shape, jnp.bfloat16), jnp.zeros(span_state.shape, jnp.bfloat16))


def states_whole(block_decay, span_state):
    return carried_in(
        (block_decay, span_state), SEQ, forward_join, neutral(block_decay, span_state), False
    )[1]


def grads_whole(block_decay, state_grad):
    return carried_in(
        (block_decay, state_grad), SEQ, backward_join, neutral(block_decay, state_grad), True
    )[1]


def on_device(mixer_in, write_proj, read_proj, dt_steps, decay_exp, norm_gain, skip_gain, out_grad):
    length = mixer_in.shape[1]
    mixed = jnp.transpose(mixer_in[0].reshape(length, G, HG, P_SIZE), (1, 2, 3, 0))
    upstream = jnp.transpose(out_grad[0].reshape(length, G, HG, P_SIZE), (1, 2, 3, 0))
    write = jnp.transpose(write_proj[0].reshape(length, G, N), (1, 2, 0))
    read = jnp.transpose(read_proj[0].reshape(length, G, N), (1, 2, 0))
    gain_whole, skip_whole = gather_together((norm_gain, skip_gain), SEQ, (0, 0))
    gain_full = gain_whole.reshape(G, HG, P_SIZE)
    skip_full = skip_whole.reshape(G, HG)
    log_decay, step_size, mixing, inner_part, ending, span_state, block_decay, readout = (
        block_front(mixed, write, read, dt_steps[0], decay_exp[0])
    )
    carried = states_whole(block_decay, span_state)
    delta_wide, delta_half, state_grad, read_part, gain_part, skip_part = block_middle(
        mixed, read, skip_full, gain_full, upstream, inner_part, readout, carried
    )
    carried_grad = grads_whole(block_decay, state_grad)
    mixer_grad, read_grad = block_back(
        mixed,
        write,
        skip_full,
        log_decay,
        step_size,
        mixing,
        ending,
        delta_wide,
        delta_half,
        read_part,
        carried_grad,
    )
    gain_flat = gain_part.reshape(H * P_SIZE)
    skip_flat = skip_part.reshape(H)
    gain_share, skip_share = (
        summed_on_arrival(gain_flat, SEQ, 0),
        summed_on_arrival(skip_flat, SEQ, 0),
    )
    gain_piece, skip_piece = (
        one_axis_at_a_time(gain_share, REP),
        one_axis_at_a_time(skip_share, REP),
    )
    mixer_rows = jnp.transpose(mixer_grad, (3, 0, 1, 2)).reshape(1, length, H * P_SIZE)
    read_rows = jnp.transpose(read_grad, (2, 0, 1)).reshape(1, length, G * N)
    return (mixer_rows, read_rows, gain_piece, skip_piece)


def solution(mesh):
    split = Mesh(mesh.devices.reshape(4, 4, 32, 2), ("seq_0", "seq_1", "rep_0", "rep_1"))
    return jax.shard_map(
        on_device,
        mesh=split,
        in_specs=(
            P(REP, SEQ, None),
            P(REP, SEQ, None),
            P(REP, SEQ, None),
            P(REP, SEQ, None),
            P(REP, SEQ, None),
            P(SEQ),
            P(SEQ),
            P(REP, SEQ, None),
        ),
        out_specs=(P(REP, SEQ, None), P(REP, SEQ, None), P(SEQ), P(SEQ)),
        check_vma=False,
    )
```

profile of v0, /device:TPU:1, one launch (start us, length us, event | category | flops | bytes accessed | tf_op | source)
XLA Modules:
  0.0 395.2 jit_solution(12612043344823148222)
XLA Ops:
  7.2 0.8 convert_multiply_fusion.3
  8.1 2.2 reduce_window_sum.11
  10.3 1.0 copy.77
  11.8 0.9 exponential_bitcast_fusion
  12.7 0.7 copy.61
  13.4 1.4 convolution_convert_fusion.1
  14.9 9.3 %all-gather = bf16[16,16,1]{1,2,0:T(2,128)(2,1)S(1)} all-gather(bf16[4,16,1]{1,2,0:T(2,128)(2,1)S(1)} %copy.63), channel_id=2, replica_groups=mesh['seq_0'=4,'seq_1'=4,'rep_0'=32,'rep_1'=2] {'seq_1'}, dimensions={0}, use_global_device_ids=true | all-gather | bytes 640 | tf_op jit(solution)/shard_map/all_gather | solution.py:29
  24.2 0.6 broadcast_select_fusion
  24.8 64.4 %all-gather.13.cloned.1.call-done = bf16[16,16,64,128]{3,2,1,0:T(8,128)(2,1)} async-done(((bf16[4,16,64,128]{3,2,1,0:T(8,128)(2,1)}), bf16[16,16,64,128]{3,2,1,0:T(8,128)(2,1)}) %all-gather.13.cloned.1.call-update) | async-done | bytes 4194320 | tf_op jit(solution)/shard_map/all_gather | solution.py:29
  89.2 3.7 fusion.10
  93.1 1.3 dynamic-slice
  95.1 59.5 %all-reduce = f32[4160]{0:T(1024)S(1)} all-reduce(f32[4160]{0:T(1024)S(1)} %maximum_dynamic-update-slice_fusion), channel_id=4, replica_groups=mesh['seq_0'=4,'seq_1'=4,'rep_0'=32,'rep_1'=2] {'seq_0','seq_1'}, use_global_device_ids=true, to_apply=%add | all-reduce | flops 4160 | bytes 33280
  154.8 0.7 copy.59
  155.5 0.7 mul.433
  156.1 0.7 mul.438
  157.0 0.7 copy.62
  157.7 1.5 copy.66
  159.7 5.2 %all_gather.41 = bf16[4,4,16]{2,1,0:T(4,128)(2,1)S(1)} all-gather(bf16[1,4,16]{2,1,0:T(4,128)(2,1)S(1)} %get-tuple-element.48), channel_id=1, replica_groups=mesh['seq_0'=4,'seq_1'=4,'rep_0'=32,'rep_1'=2] {'seq_0'}, dimensions={0}, use_global_device_ids=true | all-gather | bytes 640 | tf_op jit(solution)/shard_map/all_gather | solution.py:29
  166.1 1.3 fusion.97
  167.4 1.1 fusion.112
  168.5 0.7 copy-done.12
  169.2 4.3 %fusion.46 = f32[4,16,128,64]{2,3,1,0:T(8,128)} fusion(bf16[4,16,64,128]{3,2,1,0:T(8,128)(2,1)S(1)} %bitcast.281, f32[4,16,128]{2,1,0:T(8,128)} %bitcast.297, f32[4,16,128]{2,1,0:T(8,128)} %copy.59, f32[4,128,128]{2,1,0:T(8,128)S(1)} %fusion.112, pred[128,128]{1,0:T(8,128)(4,1)S(1)} %iota_compare_fusion), kind=kOutput, calls=%fused_computation.86 | convolution fusion | flops 140509184 | bytes 3489792 | tf_op jit(solution)/shard_map/gjts,gjps->gjpt/dot_general | solution.py:72
  173.6 7.3 %add_convert_fusion.1 = bf16[4,16,64,128]{3,2,1,0:T(8,128)(2,1)S(1)} fusion(bf16[4,4,16,64,128]{4,3,2,1,0:T(8,128)(2,1)} %all-gather.9.cloned.1.call-done, f32[4,16]{1,0:T(4,128)} %copy-done.19, f32[4,16]{1,0:T(4,128)S(1)} %bitcast.309, f32[4,16]{1,0:T(4,128)S(1)} %bitcast.303, f32[4,16]{1,0:T(4,128)S(1)} %bitcast.315, f32[4,16]{1,0:T(4,128)} %multiply_bitcast_fusion.1, ...), kind=kLoop, calls=%fused_computation.84 | loop fusion | flops 25690112 | bytes 9439496 | tf_op jit(solution)/shard_map/convert_element_type | solution.py:156
  180.9 2.0 multiply_reduce_fusion.3
  183.5 1.9 multiply_reduce_fusion.1
  186.0 2.0 fusion.26
  188.0 1.3 copy-done
  189.3 1.4 convolution_convert_fusion
  190.8 79.8 %all-gather.15.cloned.1.call-done = bf16[16,16,64,128]{3,2,1,0:T(8,128)(2,1)} async-done(((bf16[4,16,64,128]{3,2,1,0:T(8,128)(2,1)}), bf16[16,16,64,128]{3,2,1,0:T(8,128)(2,1)}) %all-gather.15.cloned.1.call-update) | async-done | bytes 4194320 | tf_op jit(solution)/shard_map/all_gather | solution.py:29
  270.6 3.6 fusion.13
  274.3 1.0 copy.68
  275.4 8.0 %all_gather.50 = bf16[4,4,16]{2,1,0:T(4,128)(2,1)S(1)} all-gather(bf16[1,4,16]{2,1,0:T(4,128)(2,1)} %get-tuple-element.47), channel_id=1, replica_groups=mesh['seq_0'=4,'seq_1'=4,'rep_0'=32,'rep_1'=2] {'seq_0'}, dimensions={0}, use_global_device_ids=true | all-gather | bytes 640 | tf_op jit(solution)/shard_map/all_gather | solution.py:29
  284.0 0.6 fusion.100
  284.6 1.3 all_to_all.14
  285.9 3.6 all-to-all-start.1
  289.5 4.1 %fusion.45 = f32[4,16,64,128]{3,2,1,0:T(8,128)} fusion(f32[4,16,128]{2,1,0:T(8,128)S(1)} %bitcast.298, f32[4,16,128]{2,1,0:T(8,128)S(1)} %copy-done.17, f32[4,128,128]{2,1,0:T(8,128)} %copy-done.12, pred[128,128]{1,0:T(8,128)(4,1)} %copy-done.20, f32[4,16,64,128]{3,2,1,0:T(8,128)} %copy-done), kind=kOutput, calls=%fused_computation.85 | convolution fusion | flops 141033472 | bytes 4538368 | tf_op jit(solution)/shard_map/gjts,gjpt->gjps/dot_general | solution.py:72
  293.6 2.9 multiply_reduce_fusion
  296.6 1.2 convolution_bitcast_fusion.1
  297.8 0.7 all_to_all.12
  299.1 6.5 %all-to-all-start = ((f32[16,1,256]{2,1,0:T(1,128)}), f32[16,1,256]{2,1,0:T(1,128)S(1)}, u32[]{:S(2)}, u32[]{:S(2)}) async-start(f32[16,1,256]{2,1,0:T(1,128)} %all_to_all.12), calls=%async_computation | async-start | bytes 32768 | tf_op jit(solution)/shard_map/all_to_all | solution.py:63
  305.6 1.2 fusion.48
  306.8 0.8 copy.71
  307.6 0.7 reduce_sum.69
  308.3 3.5 all-to-all-done
  311.9 49.3 %all-reduce.1 = (f32[256]{0:T(256)S(1)}, f32[4]{0:T(128)S(1)}) all-reduce(f32[256]{0:T(256)S(1)} %reduce_sum.67, f32[4]{0:T(128)S(1)} %reduce_sum.69), channel_id=1, replica_groups=mesh['seq_0'=4,'seq_1'=4,'rep_0'=32,'rep_1'=2] {'rep_0'}, use_global_device_ids=true, to_apply=%region_6.7 | all-reduce | flops 260 | bytes 2080 | tf_op jit(solution)/shard_map/psum | solution.py:68
  361.2 17.3 %all-reduce.2 = (f32[256]{0:T(256)}, f32[4]{0:T(128)}) all-reduce(f32[256]{0:T(256)S(1)} %get-tuple-element.26, f32[4]{0:T(128)S(1)} %get-tuple-element.27), channel_id=1, replica_groups=mesh['seq_0'=4,'seq_1'=4,'rep_0'=32,'rep_1'=2] {'rep_1'}, use_global_device_ids=true, to_apply=%region_7.8 | all-reduce | flops 260 | bytes 2080 | tf_op jit(solution)/shard_map/psum | solution.py:68
  378.6 7.8 %fusion.43 = bf16[128,4,16,64]{0,3,2,1:T(8,128)(2,1)} fusion(f32[4,16,64,128]{3,2,1,0:T(8,128)} %get-tuple-element.59, f32[4,16,128,64]{2,3,1,0:T(8,128)} %fusion.46, f32[4,16,64,128]{3,2,1,0:T(8,128)} %fusion.45, bf16[128,4,16,64]{0,3,2,1:T(8,128)(2,1)S(1)} %bitcast.285, f32[128,4,16,64]{0,3,2,1:T(8,128)S(1)} %bitcast.279, ...), kind=kOutput, calls=%fused_computation.74 | convolution fusion | flops 167772160 | bytes 19094024 | tf_op jit(solution)/shard_map/gns,gjpn->gjps/dot_general | solution.py:72
  386.4 2.3 copy.70
  (95 shorter events, 5.3 us)
Async XLA Ops:
  7.2 5.6 %copy-start.7 = (bf16[1,128,4096]{2,1,0:T(8,128)(2,1)S(1)}, bf16[1,128,4096]{2,1,0:T(8,128)(2,1)}, u32[]{:S(2)}) copy-start(bf16[1,128,4096]{2,1,0:T(8,128)(2,1)} %param.8) | copy-start | bytes 3145732
  7.2 82.1 %all-gather.13.cloned.1.call-start = ((), (), s32[]{:S(2)}) async-start(), calls=%async_computation.4 | async-start | bytes 5242880 | tf_op jit(solution)/shard_map/all_gather | solution.py:29
  8.1 3.7 copy-start.14
  11.3 2.1 copy-start.4
  14.9 158.7 %all-gather.9.cloned.1.call-start = ((), (), s32[]{:S(2)}) async-start(), calls=%async_computation.2 | async-start | bytes 5242880 | tf_op jit(solution)/shard_map/all_gather | solution.py:29
  24.8 68.1 %copy-start.19 = (f32[4,16]{1,0:T(4,128)}, f32[4,16]{1,0:T(4,128)S(1)}, u32[]{:S(2)}) copy-start(f32[4,16]{1,0:T(4,128)S(1)} %broadcast_multiply_fusion.2) | copy-start | bytes 772
  89.2 5.8 %copy-start.29 = (f32[256]{0:T(256)S(1)}, f32[256]{0:T(256)}, u32[]{:S(2)}) copy-start(f32[256]{0:T(256)} %param.13) | copy-start | bytes 3076
  89.2 5.8 %copy-start.30 = (f32[4]{0:T(128)S(1)}, f32[4]{0:T(128)}, u32[]{:S(2)}) copy-start(f32[4]{0:T(128)} %param.14) | copy-start | bytes 52
  89.2 67.6 %copy-start.16 = (bf16[1,128,512]{2,1,0:T(8,128)(2,1)S(1)}, bf16[1,128,512]{2,1,0:T(8,128)(2,1)}, u32[]{:S(2)}) copy-start(bf16[1,128,512]{2,1,0:T(8,128)(2,1)} %param.10) | copy-start | bytes 393220
  93.0 177.6 %all-gather.15.cloned.1.call-start = ((), (), s32[]{:S(2)}) async-start(), calls=%async_computation.5 | async-start | bytes 5242880 | tf_op jit(solution)/shard_map/all_gather | solution.py:29
  165.0 3.5 copy-start.20
  168.5 0.7 copy-start.12
  173.6 7.3 %copy-start.6 = (f32[4,16,128,64]{2,3,1,0:T(8,128)S(1)}, f32[4,16,128,64]{2,3,1,0:T(8,128)}, u32[]{:S(2)}) copy-start(f32[4,16,128,64]{2,3,1,0:T(8,128)} %fusion.46) | copy-start | bytes 6291460
  173.6 7.3 %copy-start.8 = (f32[4,16,128]{2,1,0:T(8,128)S(1)}, f32[4,16,128]{2,1,0:T(8,128)}, u32[]{:S(2)}) copy-start(f32[4,16,128]{2,1,0:T(8,128)} %copy.62) | copy-start | bytes 98308
  173.6 7.3 %copy-start.24 = (f32[4,16]{1,0:T(4,128)S(1)}, f32[4,16]{1,0:T(4,128)}, u32[]{:S(2)}) copy-start(f32[4,16]{1,0:T(4,128)} %mul.433) | copy-start | bytes 772
  180.9 2.0 copy-start.2
  180.9 2.6 copy-start.10
  188.0 1.3 copy-start
  190.7 187.8 %all-gather.11.cloned.1.call-start = ((), (), s32[]{:S(2)}) async-start(), calls=%async_computation.3 | async-start | bytes 5242880 | tf_op jit(solution)/shard_map/all_gather | solution.py:29
  190.8 83.4 %copy-start.22 = (f32[4,16]{1,0:T(4,128)}, f32[4,16]{1,0:T(4,128)S(1)}, u32[]{:S(2)}) copy-start(f32[4,16]{1,0:T(4,128)S(1)} %broadcast_multiply_fusion.1) | copy-start | bytes 772
  190.8 98.7 %copy-start.15 = (f32[1,128,64]{1,2,0:T(8,128)S(1)}, f32[1,128,64]{1,2,0:T(8,128)}, u32[]{:S(2)}) copy-start(f32[1,128,64]{1,2,0:T(8,128)} %copy-done.14) | copy-start | bytes 98308
  190.8 98.7 %copy-start.17 = (f32[4,16,128]{2,1,0:T(8,128)S(1)}, f32[4,16,128]{2,1,0:T(8,128)}, u32[]{:S(2)}) copy-start(f32[4,16,128]{2,1,0:T(8,128)} %copy.59) | copy-start | bytes 98308
  285.9 12.6 %all-to-all-start.1 = ((f32[16,1,4]{2,1,0:T(1,128)}), f32[16,1,4]{2,1,0:T(1,128)S(1)}, u32[]{:S(2)}, u32[]{:S(2)}) async-start(f32[16,1,4]{2,1,0:T(1,128)} %bitcast.77), calls=%async_computation.1 | async-start | bytes 16384 | tf_op jit(solution)/shard_map/all_to_all | solution.py:63
  289.5 4.1 %copy-start.1 = (f32[4,16,64,128]{3,2,1,0:T(8,128)S(1)}, f32[4,16,64,128]{3,2,1,0:T(8,128)}, u32[]{:S(2)}) copy-start(f32[4,16,64,128]{3,2,1,0:T(8,128)} %copy-done) | copy-start | bytes 6291460
  289.5 4.1 %copy-start.21 = (pred[128,128]{1,0:T(8,128)(4,1)S(1)}, pred[128,128]{1,0:T(8,128)(4,1)}, u32[]{:S(2)}) copy-start(pred[128,128]{1,0:T(8,128)(4,1)} %copy-done.20) | copy-start | bytes 49156
  293.6 2.9 copy-start.3
  293.6 2.9 copy-start.9
  296.5 1.3 copy-start.13
  296.5 9.1 %copy-start.5 = (bf16[1,128,512]{1,2,0:T(8,128)(2,1)S(1)}, bf16[1,128,512]{1,2,0:T(8,128)(2,1)}, u32[]{:S(2)}) copy-start(bf16[1,128,512]{1,2,0:T(8,128)(2,1)} %copy-done.4) | copy-start | bytes 393220
  296.5 82.0 %copy-start.11 = (f32[4,16,64]{2,1,0:T(8,128)S(1)}, f32[4,16,64]{2,1,0:T(8,128)}, u32[]{:S(2)}) copy-start(f32[4,16,64]{2,1,0:T(8,128)} %mul.438) | copy-start | bytes 49156
  296.5 82.0 %copy-start.23 = (f32[4,16]{1,0:T(4,128)S(1)}, f32[4,16]{1,0:T(4,128)}, u32[]{:S(2)}) copy-start(f32[4,16]{1,0:T(4,128)} %copy-done.22) | copy-start | bytes 772
  296.5 82.0 %copy-start.25 = (f32[4,16]{1,0:T(4,128)S(1)}, f32[4,16]{1,0:T(4,128)}, u32[]{:S(2)}) copy-start(f32[4,16]{1,0:T(4,128)} %mul.433) | copy-start | bytes 772
  296.5 82.0 %copy-start.26 = (f32[4,16]{1,0:T(4,128)S(1)}, f32[4,16]{1,0:T(4,128)}, u32[]{:S(2)}) copy-start(f32[4,16]{1,0:T(4,128)} %get-tuple-element.39) | copy-start | bytes 772
  296.6 82.0 %copy-start.27 = (f32[128,4]{0,1:T(4,128)S(1)}, f32[128,4]{0,1:T(4,128)}, u32[]{:S(2)}) copy-start(f32[128,4]{0,1:T(4,128)} %get-tuple-element.55) | copy-start | bytes 6148
  296.6 82.0 %copy-start.28 = (f32[128,4]{0,1:T(4,128)S(1)}, f32[128,4]{0,1:T(4,128)}, u32[]{:S(2)}) copy-start(f32[128,4]{0,1:T(4,128)} %get-tuple-element.57) | copy-start | bytes 6148
  298.5 0.6 copy-start.18
  299.1 12.8 %all-to-all-start = ((f32[16,1,256]{2,1,0:T(1,128)}), f32[16,1,256]{2,1,0:T(1,128)S(1)}, u32[]{:S(2)}, u32[]{:S(2)}) async-start(f32[16,1,256]{2,1,0:T(1,128)} %all_to_all.12), calls=%async_computation | async-start | bytes 32768 | tf_op jit(solution)/shard_map/all_to_all | solution.py:63
Sparse Core Ops, SparseCore 0:
  15.0 74.2 all-gather.12
  93.1 67.3 all-gather.8
  190.9 79.7 all-gather.14
  274.4 66.8 all-gather.10
where the time goes:
time: 396 us; the launch traced here: 395 us
  blocking collectives  149 us (38%)
  waiting for transfers between devices  148 us (37%)
  other arithmetic  29.4 us (7%)
  matrix products  27.5 us (7%)
  local copies, waits for them, and re-layouts  16.8 us (4%)
  between operations  14.9 us (4%)
  starting transfers between devices  10.2 us (3%)
    all_gather x4, waiting for transfers between devices, carried_in(): pieces = jax.tree.map(lambda part: lax.all_gather(part, axis), total)  144 us
    psum x2, blocking collectives, one_axis_at_a_time(): return functools.reduce(lax.psum, axes, array)  66.6 us
    unnamed x1, blocking collectives  59.5 us
    dot_general x10, matrix products, contract(): return jnp.einsum(form, left, right, preferred_element_type=jnp.float32)  27.5 us
    all_gather x3, blocking collectives, carried_in(): pieces = jax.tree.map(lambda part: lax.all_gather(part, axis), total)  22.5 us
    convert_element_type x2, other arithmetic, forward_join(): state = (decay_late.astype(jnp.float32)[..., None, None] * state_early.as...  11 us
    all_to_all x2, starting transfers between devices, summed_on_arrival(): lax.all_to_all(blocks, axis, split_axis=0, concat_axis=0, tiled=True)  10.1 us
  transfers between devices with their start and end apart: 6, of which 3 were waited for; matrix products, arithmetic and copies ran while one was open for 7% of the time, Pallas kernels for 0%

commit v1 on v0

v1 whole, which is shorter than its diff:
```python
import jax
import jax.numpy as jnp
from jax import lax
from jax.experimental import pallas as pl
from jax.experimental.pallas import tpu as pltpu
from jax.sharding import Mesh
from jax.sharding import PartitionSpec as P

H = 64
P_SIZE = 64
N = 128
G = 4
HG = 16
T = 128
D = 16
HEADS = H // D
LANES = HEADS * P_SIZE
SEQ = ("seq_0", "seq_1")
F32 = jnp.float32
BF16 = jnp.bfloat16
BLOCKS_PER_STEP = 2
STEPS = D // BLOCKS_PER_STEP
FAR = -1e30


def contract(left, right, dims):
    return lax.dot_general(left, right, (dims, ((), ())), preferred_element_type=F32)


def pack_kernel(x_ref, up_ref, write_ref, read_ref, dt_ref, dec_ref, out_ref):
    dec = dec_ref[...]
    high = (dec >> 8).astype(F32)
    low = (dec & 255).astype(F32)
    steps = dt_ref[...].astype(F32)
    for j in range(4):
        cols = slice(LANES * j, LANES * (j + 1))
        out_ref[j, :T, :256] = x_ref[:, cols]
        out_ref[j, :T, 256:512] = up_ref[:, cols]
        out_ref[j, :T, 512:640] = write_ref[...]
        out_ref[j, :T, 640:768] = read_ref[...]
        base = 8 * (j // 2)
        for place, rows in enumerate((steps, high, low)):
            eight = rows[base : base + 8]
            if j % 2 == 1:
                eight = pltpu.roll(eight, 4, 0)
            out_ref[j, T:, 128 * place : 128 * (place + 1)] = eight.astype(BF16)
        out_ref[j, T:, 384:] = jnp.zeros((8, 384), BF16)


def scalars(tail):
    upto = (
        lax.broadcasted_iota(jnp.int32, (T, T), 0) <= lax.broadcasted_iota(jnp.int32, (T, T), 1)
    ).astype(F32).astype(BF16)
    step = tail[:, :128].astype(F32) / 16.0
    whole = contract(tail[:, 128:256], upto, ((1,), (0,))) * 256.0 + contract(
        tail[:, 256:384], upto, ((1,), (0,))
    )
    log_decay = -(whole / 65536.0)
    last = jnp.broadcast_to(log_decay[:, T - 1 : T], (8, T))
    ending = jnp.exp(last - log_decay) * step
    readout = jnp.exp(log_decay)
    block_decay = jnp.exp(last).astype(BF16).astype(F32)
    cols = jnp.transpose(jnp.concatenate([log_decay, step, ending, readout], axis=0))
    return log_decay, step, block_decay, cols


def low_half(shape):
    return lax.broadcasted_iota(jnp.int32, shape, len(shape) - 1) < P_SIZE


def spread(cols, at):
    mask = low_half((T, 128))
    pairs = []
    for i in range(HEADS // 2):
        a = jnp.broadcast_to(cols[:, at + 2 * i : at + 2 * i + 1], (T, 128))
        b = jnp.broadcast_to(cols[:, at + 2 * i + 1 : at + 2 * i + 2], (T, 128))
        pairs.append(jnp.where(mask, a, b))
    return jnp.concatenate(pairs, axis=1)


def spread_rows(rows):
    mask = low_half((1, 128))
    return jnp.concatenate(
        [
            jnp.where(mask, rows[2 * i : 2 * i + 1], rows[2 * i + 1 : 2 * i + 2])
            for i in range(HEADS // 2)
        ],
        axis=1,
    )


def skip_lanes(skip_ref):
    lane = lax.broadcasted_iota(jnp.int32, (1, LANES), 1) // P_SIZE
    row = jnp.full((1, LANES), skip_ref[HEADS - 1], F32)
    for j in range(HEADS - 1):
        row = jnp.where(lane == j, skip_ref[j], row)
    return row


def two_heads(pair):
    mask = low_half((T, 128))
    return jnp.concatenate(
        [jnp.where(mask, pair, 0.0).astype(BF16), jnp.where(mask, 0.0, pair).astype(BF16)], axis=0
    )


def forward_kernel(in_ref, gain_ref, skip_ref, mo_ref, carried_ref, stats_ref, carry, sums):
    step_id = pl.program_id(0)

    @pl.when(step_id == 0)
    def _():
        carry[...] = jnp.zeros_like(carry)
        sums[...] = jnp.zeros_like(sums)

    gain = gain_ref[...]
    skip = skip_lanes(skip_ref)
    row_id = lax.broadcasted_iota(jnp.int32, (T, T), 0)
    lane_id = lax.broadcasted_iota(jnp.int32, (T, T), 1)
    causal = row_id >= lane_id
    state = carry[...]
    found = sums[...]
    results = []
    for b in range(BLOCKS_PER_STEP):
        x = in_ref[b, :T, :256].astype(F32)
        up = in_ref[b, :T, 256:512].astype(F32)
        write = in_ref[b, :T, 512:640]
        read = in_ref[b, :T, 640:768]
        log_decay, step, block_decay, cols = scalars(in_ref[b, T:, :])
        scores = contract(read, write, ((1,), (1,)))
        inner = []
        for i in range(HEADS // 2):
            mixing = []
            for j in (2 * i, 2 * i + 1):
                gap = jnp.where(causal, cols[:, j : j + 1] - log_decay[j : j + 1], FAR)
                mixing.append((scores * (jnp.exp(gap) * step[j : j + 1])).astype(BF16))
            inner.append(
                contract(
                    jnp.concatenate(mixing, axis=1),
                    two_heads(x[:, 128 * i : 128 * (i + 1)]),
                    ((1,), (0,)),
                )
            )
        weighted = (x * spread(cols, 16)).astype(BF16)
        span_state = contract(write, weighted, ((0,), (0,))).astype(BF16).astype(F32)
        carried = state.astype(BF16)
        state = (spread_rows(block_decay) * state + span_state).astype(BF16).astype(F32)
        out = (
            jnp.concatenate(inner, axis=1)
            + spread(cols, 24) * contract(read, carried, ((1,), (0,)))
            + skip * x
        )
        square = jnp.sum(out * out, axis=1, keepdims=True)
        cross = jnp.sum(up * gain * out, axis=1, keepdims=True)
        at = 2 * (BLOCKS_PER_STEP * step_id + b)
        found = jnp.where(lane_id == at, square, jnp.where(lane_id == at + 1, cross, found))
        results.append((out, carried))
    for b, (out, carried) in enumerate(results):
        mo_ref[b] = out
        carried_ref[b] = carried
    carry[...] = state
    sums[...] = found

    @pl.when(step_id == STEPS - 1)
    def _():
        rows = jnp.transpose(sums[...])[: 2 * D]
        for d in range(4):
            stats_ref[d] = rows


def backward_kernel(
    in_ref, mo_ref, carried_ref, stats_ref, gain_ref, skip_ref, out_ref, part_ref, carry, sums, parts
):
    step_id = pl.program_id(0)

    @pl.when(step_id == 0)
    def _():
        carry[...] = jnp.zeros_like(carry)
        parts[...] = jnp.zeros_like(parts)
        total = stats_ref[0] + stats_ref[1] + stats_ref[2] + stats_ref[3]
        sums[...] = jnp.transpose(jnp.concatenate([total] * 4, axis=0))

    gain = gain_ref[...]
    skip = skip_lanes(skip_ref)
    row_id = lax.broadcasted_iota(jnp.int32, (T, T), 0)
    lane_id = lax.broadcasted_iota(jnp.int32, (T, T), 1)
    later = row_id <= lane_id
    state = carry[...]
    gain_sum = parts[0:1]
    skip_sum = parts[1:2]
    results = []
    first = BLOCKS_PER_STEP * (STEPS - 1 - step_id)
    found = sums[...]
    for b in reversed(range(BLOCKS_PER_STEP)):
        x = in_ref[b, :T, :256].astype(F32)
        up = in_ref[b, :T, 256:512].astype(F32)
        write = in_ref[b, :T, 512:640]
        read = in_ref[b, :T, 640:768]
        out = mo_ref[b]
        log_decay, step, block_decay, cols = scalars(in_ref[b, T:, :])
        here = pltpu.roll(found, lax.rem(128 - 2 * (first + b), 128), 1)
        inverse = lax.rsqrt(here[:, 0:1] / (HG * P_SIZE) + 1e-05)
        mean = inverse * here[:, 1:2] / (HG * P_SIZE)
        normed = out * inverse
        delta = inverse * (up * gain - normed * mean)
        gain_sum = gain_sum + jnp.sum(up * normed, axis=0, keepdims=True)
        skip_sum = skip_sum + jnp.sum(delta * x, axis=0, keepdims=True)
        scaled = (delta * spread(cols, 24)).astype(BF16)
        half = delta.astype(BF16)
        scores = contract(write, read, ((1,), (1,)))
        score_grad = jnp.zeros((T, T), F32)
        mixed = []
        for i in range(HEADS // 2):
            pair = slice(128 * i, 128 * (i + 1))
            mix_grad = contract(two_heads(x[:, pair]), half[:, pair], ((1,), (1,)))
            mixing = []
            for n, j in enumerate((2 * i, 2 * i + 1)):
                gap = jnp.where(later, log_decay[j : j + 1] - cols[:, j : j + 1], FAR)
                weight = jnp.exp(gap) * cols[:, 8 + j : 9 + j]
                mixing.append((scores * weight).astype(BF16))
                score_grad = score_grad + weight * mix_grad[T * n : T * (n + 1)]
            mixed.append(
                contract(
                    jnp.concatenate(mixing, axis=1), two_heads(delta[:, pair]), ((1,), (0,))
                )
            )
        carried_grad = state.astype(BF16)
        mixer_grad = (
            jnp.concatenate(mixed, axis=1)
            + spread(cols, 16) * contract(write, carried_grad, ((1,), (0,)))
            + skip * delta
        )
        read_grad = contract(score_grad.astype(BF16), write, ((0,), (0,))) + contract(
            scaled, carried_ref[b], ((1,), (1,))
        )
        state_grad = contract(read, scaled, ((0,), (0,))).astype(BF16).astype(F32)
        state = (state_grad + spread_rows(block_decay) * state).astype(BF16).astype(F32)
        results.append((b, mixer_grad, read_grad))
    for b, mixer_grad, read_grad in results:
        out_ref[b, :, :256] = mixer_grad.astype(BF16)
        out_ref[b, :, 256:] = read_grad.astype(BF16)
    carry[...] = state
    parts[0:1] = gain_sum
    parts[1:2] = skip_sum

    @pl.when(step_id == STEPS - 1)
    def _():
        part_ref[0:1] = parts[0:1]
        part_ref[1:2] = parts[1:2]


def unpack_kernel(in_ref, mixer_ref, read_ref):
    total = jnp.zeros((T, 128), F32)
    for j in range(4):
        mixer_ref[:, LANES * j : LANES * (j + 1)] = in_ref[j, :, :256]
        total = total + in_ref[j, :, 256:].astype(F32)
    read_ref[...] = total.astype(BF16)


def whole(shape):
    return pl.BlockSpec(shape, lambda i: (0,) * len(shape))


SCALARS = pl.BlockSpec(memory_space=pltpu.SMEM)


def call(kernel, grid, in_specs, out_specs, out_shape, scratch=(), flops=0, interpret=False):
    return pl.pallas_call(
        kernel,
        grid=(grid,),
        in_specs=in_specs,
        out_specs=out_specs,
        out_shape=out_shape,
        scratch_shapes=scratch,
        cost_estimate=pl.CostEstimate(flops=flops, bytes_accessed=1 << 20, transcendentals=0),
        interpret=interpret,
    )


def shape(dims, dtype):
    return jax.ShapeDtypeStruct(dims, dtype)


def build(interpret):
    def on_device(mixer_in, write_proj, read_proj, dt_steps, decay_exp, norm_gain, skip_gain, out_grad):
        def exchange(array, axes):
            return lax.all_to_all(array, axes, split_axis=0, concat_axis=0, tiled=True)

        gain = norm_gain.reshape(1, LANES)
        column = lambda i: (0, i)
        sent = call(
            pack_kernel,
            G,
            [
                pl.BlockSpec((T, 1024), column),
                pl.BlockSpec((T, 1024), column),
                pl.BlockSpec((T, N), column),
                pl.BlockSpec((T, N), column),
                pl.BlockSpec((HG, T), lambda i: (i, 0)),
                pl.BlockSpec((HG, T), lambda i: (i, 0)),
            ],
            pl.BlockSpec((4, T + 8, 768), lambda i: (i, 0, 0)),
            shape((D, T + 8, 768), BF16),
            interpret=interpret,
        )(
            mixer_in[0],
            out_grad[0],
            write_proj[0],
            read_proj[0],
            jnp.transpose(dt_steps[0]),
            jnp.transpose(decay_exp[0]),
        )
        blocks = exchange(sent, SEQ)

        along = lambda i: (i, 0, 0)
        size = BLOCKS_PER_STEP
        mixer_out, carried, stats = call(
            forward_kernel,
            STEPS,
            [pl.BlockSpec((size, T + 8, 768), along), whole((1, LANES)), SCALARS],
            [
                pl.BlockSpec((size, T, LANES), along),
                pl.BlockSpec((size, N, LANES), along),
                whole((4, 2 * D, T)),
            ],
            [
                shape((D, T, LANES), F32),
                shape((D, N, LANES), BF16),
                shape((4, 2 * D, T), F32),
            ],
            [pltpu.VMEM((N, LANES), F32), pltpu.VMEM((T, T), F32)],
            interpret=interpret,
        )(blocks, gain, skip_gain)
        stats = exchange(stats, "seq_1")

        back = lambda i: (STEPS - 1 - i, 0, 0)
        grads, parts = call(
            backward_kernel,
            STEPS,
            [
                pl.BlockSpec((size, T + 8, 768), back),
                pl.BlockSpec((size, T, LANES), back),
                pl.BlockSpec((size, N, LANES), back),
                whole((4, 2 * D, T)),
                whole((1, LANES)),
                SCALARS,
            ],
            [pl.BlockSpec((size, T, 384), back), whole((2, LANES))],
            [shape((D, T, 384), BF16), shape((2, LANES), F32)],
            [pltpu.VMEM((N, LANES), F32), pltpu.VMEM((T, T), F32), pltpu.VMEM((8, LANES), F32)],
            interpret=interpret,
        )(blocks, mixer_out, carried, stats, gain, skip_gain)
        grads = exchange(grads, SEQ)

        for axis in ("core", "z_low"):
            if lax.axis_size(axis) == 2:
                parts = parts + lax.ppermute(parts, axis, [(0, 1), (1, 0)])
        far = lax.axis_size("z_high")
        if far > 1:
            copies = jnp.broadcast_to(parts[None], (far, 2, LANES))
            parts = jnp.sum(exchange(copies, "z_high"), axis=0)
        mixer_grad, read_grad = call(
            unpack_kernel,
            G,
            [pl.BlockSpec((4, T, 384), along)],
            [pl.BlockSpec((T, 1024), column), pl.BlockSpec((T, N), column)],
            [shape((T, H * P_SIZE), BF16), shape((T, G * N), BF16)],
            interpret=interpret,
        )(grads)
        return (
            mixer_grad[None],
            read_grad[None],
            parts[0],
            jnp.sum(parts[1].reshape(HEADS, P_SIZE), axis=1),
        )

    return on_device


def sharded(mesh, interpret=False):
    rep = ("z_high", "z_low", "core")
    big = P(rep, SEQ, None)
    return jax.shard_map(
        build(interpret),
        mesh=mesh,
        in_specs=(big, big, big, big, big, P(SEQ), P(SEQ), big),
        out_specs=(big, big, P(SEQ), P(SEQ)),
        check_vma=False,
    )


def solution(mesh):
    names = ("seq_0", "seq_1", "z_high", "z_low", "core")
    return sharded(Mesh(mesh.devices.reshape(4, 4, 16, 2, 2), names))
```

time: 396 us -> 182 us (0.46)
  waiting for transfers between devices: 148 us -> 21.2 us
  blocking collectives: 149 us -> 95.9 us
  Pallas kernels: 0 us -> 36.8 us
  other arithmetic: 29.4 us -> 1.35 us
  matrix products: 27.5 us -> 0 us
  local copies, waits for them, and re-layouts: 16.8 us -> 1.82 us
  between operations: 14.9 us -> 0.67 us
  starting transfers between devices: 10.2 us -> 21.4 us
    all_gather x4 -> x0, waiting for transfers between devices: 144 us -> none  [carried_in(): pieces = jax.tree.map(lambda part: lax.all_gather(part, axis), total)]
    all_to_all x0 -> x3, blocking collectives: none -> 95.9 us  [exchange(): return lax.all_to_all(array, axes, split_axis=0, concat_axis=0, tiled=True)]
    psum x2 -> x0, blocking collectives: 66.6 us -> none  [one_axis_at_a_time(): return functools.reduce(lax.psum, axes, array)]
    unnamed x1 -> x0, blocking collectives: 59.5 us -> none
    pallas_call x0 -> x4, Pallas kernels: none -> 36.8 us  [the longest x1 15.6 us: on_device(): call(backward_kernel, STEPS, [pl.BlockSpec((size, T + 8, 768), back), pl....]
    dot_general x10 -> x0, matrix products: 27.5 us -> none  [contract(): return jnp.einsum(form, left, right, preferred_element_type=jnp.float32)]
    all_gather x3 -> x0, blocking collectives: 22.5 us -> none  [carried_in(): pieces = jax.tree.map(lambda part: lax.all_gather(part, axis), total)]
    ppermute x0 -> x2, starting transfers between devices: none -> 17.7 us  [on_device(): parts = parts + lax.ppermute(parts, axis, [(0, 1), (1, 0)])]
  transfers between devices with their start and end apart: 6 -> 3, of which waited for: 3 -> 3; matrix products, arithmetic and copies ran while one was open for 7% -> 1% of each run, Pallas kernels for 0% -> 0%
where the time goes in v1:
time: 182 us; the launch traced here: 179 us
  blocking collectives  95.9 us (53%)
  Pallas kernels  36.8 us (20%)
  starting transfers between devices  21.4 us (12%)
  waiting for transfers between devices  21.2 us (12%)
  local copies, waits for them, and re-layouts  1.82 us (1%)
    all_to_all x3, blocking collectives, exchange(): return lax.all_to_all(array, axes, split_axis=0, concat_axis=0, tiled=True)  95.9 us
    all_to_all x1, waiting for transfers between devices, exchange(): return lax.all_to_all(array, axes, split_axis=0, concat_axis=0, tiled=True)  18.5 us
    ppermute x2, starting transfers between devices, on_device(): parts = parts + lax.ppermute(parts, axis, [(0, 1), (1, 0)])  17.7 us
    pallas_call x1, Pallas kernels, on_device(): call(backward_kernel, STEPS, [pl.BlockSpec((size, T + 8, 768), back), pl....  15.6 us
    pallas_call x1, Pallas kernels, on_device(): call(forward_kernel, STEPS, [pl.BlockSpec((size, T + 8, 768), along), who...  13.5 us
    pallas_call x1, Pallas kernels, on_device(): call(pack_kernel, G, [pl.BlockSpec((T, 1024), column), pl.BlockSpec((T, 1...  4.14 us
    all_to_all x1, starting transfers between devices, exchange(): return lax.all_to_all(array, axes, split_axis=0, concat_axis=0, tiled=True)  3.71 us
  transfers between devices with their start and end apart: 3, of which 3 were waited for; matrix products, arithmetic and copies ran while one was open for 1% of the time, Pallas kernels for 0%

profile of v1, /device:TPU:1, one launch (start us, length us, event | category | flops | bytes accessed | tf_op | source)
XLA Modules:
  0.0 179.1 jit_solution(13649602802407774072)
XLA Ops:
  0.6 4.1 %shard_map.111 = bf16[16,136,768]{2,1,0:T(8,128)(2,1)} custom-call(bf16[128,4096]{1,0:T(8,128)(2,1)} %bitcast.14, bf16[128,4096]{1,0:T(8,128)(2,1)} %bitcast.15, bf16[128,512]{1,0:T(8,128)(2,1)} %bitcast.16, bf16[128,512]{1,0:T(8,128)(2,1)} %bitcast.17, s32[64,128]{1,0:T(8,128)} %bitcast.18, s32[64,128]{1,0:T(8,128)} %bitcast.19), custom_call_target="tpu_custom_call" | custom-call | bytes 1048576 | tf_op jit(solution)/shard_map/pallas_call | solution.py:290
  4.8 39.3 %all_to_all.20.in_ref = bf16[16,136,768]{2,1,0:T(8,128)(2,1)} all-to-all(bf16[16,136,768]{2,1,0:T(8,128)(2,1)} %shard_map.111), channel_id=1, replica_groups=mesh['seq_0'=4,'seq_1'=4,'z_high'=16,'z_low'=2,'core'=2] {'seq_0','seq_1'}, dimensions={0} | all-to-all | bytes 6684672 | tf_op jit(solution)/shard_map/all_to_all | solution.py:286
  44.0 13.5 %shard_map.112 = (f32[16,128,256]{2,1,0:T(8,128)}, bf16[16,128,256]{2,1,0:T(8,128)(2,1)}, f32[4,32,128]{2,1,0:T(8,128)}) custom-call(bf16[16,136,768]{2,1,0:T(8,128)(2,1)} %all_to_all.20.in_ref, f32[1,256]{1,0:T(1,128)} %bitcast.20, f32[4]{0:T(128)} %skip_ref.3), custom_call_target="tpu_custom_call" | custom-call | bytes 1048576 | tf_op jit(solution)/shard_map/pallas_call | solution.py:316
  57.6 8.4 %all_to_all.21.stats_ref = f32[4,32,128]{2,1,0:T(8,128)} all-to-all(f32[4,32,128]{2,1,0:T(8,128)} %get-tuple-element.13), channel_id=1, replica_groups=mesh['seq_0'=4,'seq_1'=4,'z_high'=16,'z_low'=2,'core'=2] {'seq_1'}, dimensions={0} | all-to-all | bytes 131072 | tf_op jit(solution)/shard_map/all_to_all | solution.py:286
  66.0 15.6 %shard_map.113 = (bf16[16,128,384]{2,1,0:T(8,128)(2,1)}, f32[2,256]{1,0:T(2,128)}) custom-call(bf16[16,136,768]{2,1,0:T(8,128)(2,1)} %all_to_all.20.in_ref, f32[16,128,256]{2,1,0:T(8,128)} %get-tuple-element.11.mo_ref, bf16[16,128,256]{2,1,0:T(8,128)(2,1)} %get-tuple-element.12.carried_ref, f32[4,32,128]{2,1,0:T(8,128)} %all_to_all.21.stats_ref, ...), custom_call_target="tpu_custom_call" | custom-call | bytes 1048576 | tf_op jit(solution)/shard_map/pallas_call | solution.py:336
  81.6 15.1 %collective-permute-start = (f32[2,256]{1,0:T(2,128)}, f32[2,256]{1,0:T(2,128)S(1)}, u32[]{:S(2)}, u32[]{:S(2)}) collective-permute-start(f32[2,256]{1,0:T(2,128)} %get-tuple-element.17), channel_id=1, source_target_pairs={{0,1},{1,0},{2,3},{3,2},{4,5},{5,4},{6,7},{7,6},{8,9},{9,8},{10,11... | collective-permute-start | bytes 6152 | tf_op jit(solution)/shard_map/ppermute | solution.py:356
  96.7 1.0 collective-permute-done
  97.7 0.7 add.6
  98.4 2.6 %collective-permute-start.1 = (f32[2,256]{1,0:T(2,128)S(1)}, f32[2,256]{1,0:T(2,128)S(1)}, u32[]{:S(2)}, u32[]{:S(2)}) collective-permute-start(f32[2,256]{1,0:T(2,128)S(1)} %add.6), channel_id=1, source_target_pairs={{0,2},{2,0},{1,3},{3,1},{4,6},{6,4},{5,7},{7,5},{8,10},{10,8},{9,1... | collective-permute-start | bytes 6152 | tf_op jit(solution)/shard_map/ppermute | solution.py:356
  101.0 1.7 collective-permute-done.1
  102.7 48.2 %all_to_all.22 = f32[16,2,256]{2,1,0:T(2,128)S(1)} all-to-all(f32[16,2,256]{2,1,0:T(2,128)S(1)} %broadcast_in_dim.14), channel_id=1, replica_groups=mesh['seq_0'=4,'seq_1'=4,'z_high'=16,'z_low'=2,'core'=2] {'z_high'}, dimensions={0} | all-to-all | bytes 65536 | tf_op jit(solution)/shard_map/all_to_all | solution.py:286
  151.0 3.7 %all-to-all-start.2 = ((bf16[16,128,384]{2,1,0:T(8,128)(2,1)}), bf16[16,128,384]{2,1,0:T(8,128)(2,1)S(1)}, u32[]{:S(2)}, u32[]{:S(2)}) async-start(bf16[16,128,384]{2,1,0:T(8,128)(2,1)} %get-tuple-element.14), calls=%async_computation.2 | async-start | bytes 3145728 | tf_op jit(solution)/shard_map/all_to_all | solution.py:286
  154.7 0.6 slice_reduce_fusion
  155.3 0.1 reshape_squeeze.3
  155.4 0.6 reduce_sum.19
  156.0 18.5 %all-to-all-done.2.in_ref = bf16[16,128,384]{2,1,0:T(8,128)(2,1)S(1)} async-done(((bf16[16,128,384]{2,1,0:T(8,128)(2,1)}), bf16[16,128,384]{2,1,0:T(8,128)(2,1)S(1)}, u32[]{:S(2)}, u32[]{:S(2)}) %all-to-all-start.2) | async-done | bytes 1572896 | tf_op jit(solution)/shard_map/all_to_all | solution.py:286
  174.5 0.0 copy-start
  174.5 1.2 copy-done
  175.6 3.5 %shard_map.114 = (bf16[128,4096]{1,0:T(8,128)(2,1)}, bf16[128,512]{1,0:T(8,128)(2,1)}) custom-call(bf16[16,128,384]{2,1,0:T(8,128)(2,1)} %copy-done), custom_call_target="tpu_custom_call" | custom-call | bytes 1048576 | tf_op jit(solution)/shard_map/pallas_call | solution.py:361
  (3 shorter events, 0.0 us)
Async XLA Ops:
  81.6 16.1 %collective-permute-start = (f32[2,256]{1,0:T(2,128)}, f32[2,256]{1,0:T(2,128)S(1)}, u32[]{:S(2)}, u32[]{:S(2)}) collective-permute-start(f32[2,256]{1,0:T(2,128)} %get-tuple-element.17), channel_id=1, source_target_pairs={{0,1},{1,0},{2,3},{3,2},{4,5},{5,4},{6,7},{7,6},{8,9},{9,8},{10,11... | collective-permute-start | bytes 6152 | tf_op jit(solution)/shard_map/ppermute | solution.py:356
  98.4 4.3 %collective-permute-start.1 = (f32[2,256]{1,0:T(2,128)S(1)}, f32[2,256]{1,0:T(2,128)S(1)}, u32[]{:S(2)}, u32[]{:S(2)}) collective-permute-start(f32[2,256]{1,0:T(2,128)S(1)} %add.6), channel_id=1, source_target_pairs={{0,2},{2,0},{1,3},{3,1},{4,6},{6,4},{5,7},{7,5},{8,10},{10,8},{9,1... | collective-permute-start | bytes 6152 | tf_op jit(solution)/shard_map/ppermute | solution.py:356
  151.0 23.5 %all-to-all-start.2 = ((bf16[16,128,384]{2,1,0:T(8,128)(2,1)}), bf16[16,128,384]{2,1,0:T(8,128)(2,1)S(1)}, u32[]{:S(2)}, u32[]{:S(2)}) async-start(bf16[16,128,384]{2,1,0:T(8,128)(2,1)} %get-tuple-element.14), calls=%async_computation.2 | async-start | bytes 3145728 | tf_op jit(solution)/shard_map/all_to_all | solution.py:286
  174.5 1.2 copy-start

commit v2 on v1

--- a/solution.py
+++ b/solution.py
@@ -5,6 +5,7 @@
 from jax.experimental.pallas import tpu as pltpu
 from jax.sharding import Mesh
 from jax.sharding import PartitionSpec as P
+
 
 H = 64
 P_SIZE = 64
@@ -20,6 +21,8 @@
 BF16 = jnp.bfloat16
 BLOCKS_PER_STEP = 2
 STEPS = D // BLOCKS_PER_STEP
+PACK_STEPS = 2
+GAIN_BLOCKS = 4
 FAR = -1e30
 
 
@@ -32,12 +35,13 @@
     high = (dec >> 8).astype(F32)
     low = (dec & 255).astype(F32)
     steps = dt_ref[...].astype(F32)
-    for j in range(4):
+    for j in range(D // PACK_STEPS):
         cols = slice(LANES * j, LANES * (j + 1))
+        group = slice(N * (j // 4), N * (j // 4 + 1))
         out_ref[j, :T, :256] = x_ref[:, cols]
         out_ref[j, :T, 256:512] = up_ref[:, cols]
-        out_ref[j, :T, 512:640] = write_ref[...]
-        out_ref[j, :T, 640:768] = read_ref[...]
+        out_ref[j, :T, 512:640] = write_ref[:, group]
+        out_ref[j, :T, 640:768] = read_ref[:, group]
         base = 8 * (j // 2)
         for place, rows in enumerate((steps, high, low)):
             eight = rows[base : base + 8]
@@ -167,17 +171,59 @@
             stats_ref[d] = rows
 
 
+def shared_sums(stats_ref):
+    total = stats_ref[0] + stats_ref[1] + stats_ref[2] + stats_ref[3]
+    return jnp.transpose(jnp.concatenate([total] * 4, axis=0))
+
+
+def normalise(found, block, out, up, gain):
+    here = pltpu.roll(found, lax.rem(128 - 2 * block, 128), 1)
+    inverse = lax.rsqrt(here[:, 0:1] / (HG * P_SIZE) + 1e-05)
+    mean = inverse * here[:, 1:2] / (HG * P_SIZE)
+    normed = out * inverse
+    return normed, inverse * (up * gain - normed * mean)
+
+
+def gain_kernel(in_ref, mo_ref, stats_ref, gain_ref, part_ref, sums, parts):
+    step_id = pl.program_id(0)
+
+    @pl.when(step_id == 0)
+    def _():
+        parts[...] = jnp.zeros_like(parts)
+        sums[...] = shared_sums(stats_ref)
+
+    gain = gain_ref[...]
+    found = sums[...]
+    gain_sum = parts[0]
+    skip_sum = parts[1]
+    for b in range(GAIN_BLOCKS):
+        x = in_ref[b, :, :256].astype(F32)
+        up = in_ref[b, :, 256:].astype(F32)
+        normed, delta = normalise(found, GAIN_BLOCKS * step_id + b, mo_ref[b], up, gain)
+        gain_sum = gain_sum + jnp.sum((up * normed).reshape(T // 8, 8, LANES), axis=0)
+        skip_sum = skip_sum + jnp.sum((delta * x).reshape(T // 8, 8, LANES), axis=0)
+    parts[0] = gain_sum
+    parts[1] = skip_sum
+
+    @pl.when(step_id == D // GAIN_BLOCKS - 1)
+    def _():
+        total = jnp.concatenate(
+            [jnp.sum(parts[0], axis=0, keepdims=True), jnp.sum(parts[1], axis=0, keepdims=True)],
+            axis=0,
+        )
+        for copy in range(part_ref.shape[0]):
+            part_ref[copy] = total
+
+
 def backward_kernel(
-    in_ref, mo_ref, carried_ref, stats_ref, gain_ref, skip_ref, out_ref, part_ref, carry, sums, parts
+    in_ref, mo_ref, carried_ref, stats_ref, gain_ref, skip_ref, out_ref, carry, sums
 ):
     step_id = pl.program_id(0)
 
     @pl.when(step_id == 0)
     def _():
         carry[...] = jnp.zeros_like(carry)
-        parts[...] = jnp.zeros_like(parts)
-        total = stats_ref[0] + stats_ref[1] + stats_ref[2] + stats_ref[3]
-        sums[...] = jnp.transpose(jnp.concatenate([total] * 4, axis=0))
+        sums[...] = shared_sums(stats_ref)
 
     gain = gain_ref[...]
     skip = skip_lanes(skip_ref)
@@ -185,8 +231,6 @@
     lane_id = lax.broadcasted_iota(jnp.int32, (T, T), 1)
     later = row_id <= lane_id
     state = carry[...]
-    gain_sum = parts[0:1]
-    skip_sum = parts[1:2]
     results = []
     first = BLOCKS_PER_STEP * (STEPS - 1 - step_id)
     found = sums[...]
@@ -196,14 +240,8 @@
         write = in_ref[b, :T, 512:640]
         read = in_ref[b, :T, 640:768]
         out = mo_ref[b]
-        log_decay, step, block_decay, cols = scalars(in_ref[b, T:, :])
-        here = pltpu.roll(found, lax.rem(128 - 2 * (first + b), 128), 1)
-        inverse = lax.rsqrt(here[:, 0:1] / (HG * P_SIZE) + 1e-05)
-        mean = inverse * here[:, 1:2] / (HG * P_SIZE)
-        normed = out * inverse
-        delta = inverse * (up * gain - normed * mean)
-        gain_sum = gain_sum + jnp.sum(up * normed, axis=0, keepdims=True)
-        skip_sum = skip_sum + jnp.sum(delta * x, axis=0, keepdims=True)
+        log_decay, _, block_decay, cols = scalars(in_ref[b, T:, :])
+        _, delta = normalise(found, first + b, out, up, gain)
         scaled = (delta * spread(cols, 24)).astype(BF16)
         half = delta.astype(BF16)
         scores = contract(write, read, ((1,), (1,)))
@@ -239,21 +277,15 @@
         out_ref[b, :, :256] = mixer_grad.astype(BF16)
         out_ref[b, :, 256:] = read_grad.astype(BF16)
     carry[...] = state
-    parts[0:1] = gain_sum
-    parts[1:2] = skip_sum
-
-    @pl.when(step_id == STEPS - 1)
-    def _():
-        part_ref[0:1] = parts[0:1]
-        part_ref[1:2] = parts[1:2]
 
 
 def unpack_kernel(in_ref, mixer_ref, read_ref):
-    total = jnp.zeros((T, 128), F32)
-    for j in range(4):
-        mixer_ref[:, LANES * j : LANES * (j + 1)] = in_ref[j, :, :256]
-        total = total + in_ref[j, :, 256:].astype(F32)
-    read_ref[...] = total.astype(BF16)
+    for g in range(G):
+        total = jnp.zeros((T, N), F32)
+        for d in range(4 * g, 4 * g + 4):
+            mixer_ref[:, LANES * d : LANES * (d + 1)] = in_ref[d, :, :256]
+            total = total + in_ref[d, :, 256:].astype(F32)
+        read_ref[:, N * g : N * (g + 1)] = total.astype(BF16)
 
 
 def whole(shape):
@@ -281,7 +313,7 @@
 
 
 def build(interpret):
-    def on_device(mixer_in, write_proj, read_proj, dt_steps, decay_exp, norm_gain, skip_gain, out_grad):
+    def mixer(mixer_in, write_proj, read_proj, dt_steps, decay_exp, norm_gain, skip_gain, out_grad):
         def exchange(array, axes):
             return lax.all_to_all(array, axes, split_axis=0, concat_axis=0, tiled=True)
 
@@ -289,16 +321,16 @@
         column = lambda i: (0, i)
         sent = call(
             pack_kernel,
-            G,
+            PACK_STEPS,
             [
-                pl.BlockSpec((T, 1024), column),
-                pl.BlockSpec((T, 1024), column),
-                pl.BlockSpec((T, N), column),
-                pl.BlockSpec((T, N), column),
-                pl.BlockSpec((HG, T), lambda i: (i, 0)),
-                pl.BlockSpec((HG, T), lambda i: (i, 0)),
+                pl.BlockSpec((T, H * P_SIZE // PACK_STEPS), column),
+                pl.BlockSpec((T, H * P_SIZE // PACK_STEPS), column),
+                pl.BlockSpec((T, G * N // PACK_STEPS), column),
+                pl.BlockSpec((T, G * N // PACK_STEPS), column),
+                pl.BlockSpec((H // PACK_STEPS, T), lambda i: (i, 0)),
+                pl.BlockSpec((H // PACK_STEPS, T), lambda i: (i, 0)),
             ],
-            pl.BlockSpec((4, T + 8, 768), lambda i: (i, 0, 0)),
+            pl.BlockSpec((D // PACK_STEPS, T + 8, 768), lambda i: (i, 0, 0)),
             shape((D, T + 8, 768), BF16),
             interpret=interpret,
         )(
@@ -332,8 +364,24 @@
         )(blocks, gain, skip_gain)
         stats = exchange(stats, "seq_1")
 
+        far = lax.axis_size("z_high")
+        copies = call(
+            gain_kernel,
+            D // GAIN_BLOCKS,
+            [
+                pl.BlockSpec((GAIN_BLOCKS, T, 512), along),
+                pl.BlockSpec((GAIN_BLOCKS, T, LANES), along),
+                whole((4, 2 * D, T)),
+                whole((1, LANES)),
+            ],
+            whole((far, 2, LANES)),
+            shape((far, 2, LANES), F32),
+            [pltpu.VMEM((T, T), F32), pltpu.VMEM((2, 8, LANES), F32)],
+            interpret=interpret,
+        )(blocks, mixer_out, stats, gain)
+        parts = exchange(copies, "z_high") if far > 1 else copies
         back = lambda i: (STEPS - 1 - i, 0, 0)
-        grads, parts = call(
+        grads = call(
             backward_kernel,
             STEPS,
             [
@@ -344,26 +392,21 @@
                 whole((1, LANES)),
                 SCALARS,
             ],
-            [pl.BlockSpec((size, T, 384), back), whole((2, LANES))],
-            [shape((D, T, 384), BF16), shape((2, LANES), F32)],
-            [pltpu.VMEM((N, LANES), F32), pltpu.VMEM((T, T), F32), pltpu.VMEM((8, LANES), F32)],
+            pl.BlockSpec((size, T, 384), back),
+            shape((D, T, 384), BF16),
+            [pltpu.VMEM((N, LANES), F32), pltpu.VMEM((T, T), F32)],
+            flops=1 << 34,
             interpret=interpret,
         )(blocks, mixer_out, carried, stats, gain, skip_gain)
         grads = exchange(grads, SEQ)
-
+        parts = jnp.sum(parts, axis=0)
         for axis in ("core", "z_low"):
             if lax.axis_size(axis) == 2:
                 parts = parts + lax.ppermute(parts, axis, [(0, 1), (1, 0)])
-        far = lax.axis_size("z_high")
-        if far > 1:
-            copies = jnp.broadcast_to(parts[None], (far, 2, LANES))
-            parts = jnp.sum(exchange(copies, "z_high"), axis=0)
-        mixer_grad, read_grad = call(
+        mixer_grad, read_grad = pl.pallas_call(
             unpack_kernel,
-            G,
-            [pl.BlockSpec((4, T, 384), along)],
-            [pl.BlockSpec((T, 1024), column), pl.BlockSpec((T, N), column)],
-            [shape((T, H * P_SIZE), BF16), shape((T, G * N), BF16)],
+            in_specs=[pl.BlockSpec(memory_space=pltpu.VMEM)],
+            out_shape=[shape((T, H * P_SIZE), BF16), shape((T, G * N), BF16)],
             interpret=interpret,
         )(grads)
         return (
@@ -373,7 +416,7 @@
             jnp.sum(parts[1].reshape(HEADS, P_SIZE), axis=1),
         )
 
-    return on_device
+    return mixer
 
 
 def sharded(mesh, interpret=False):
@@ -390,4 +433,5 @@
 
 def solution(mesh):
     names = ("seq_0", "seq_1", "z_high", "z_low", "core")
-    return sharded(Mesh(mesh.devices.reshape(4, 4, 16, 2, 2), names))
+    step = sharded(Mesh(mesh.devices.reshape(4, 4, 16, 2, 2), names))
+    return step

time: 182 us -> 159 us (0.87)
  the two profiles are of different devices: /device:TPU:1 before, /device:TPU:2 now
where the time goes in v2:
time: 159 us
  blocking collectives  58.5 us (37%)
  Pallas kernels  39.8 us (25%)
  starting transfers between devices  37.2 us (23%)
  waiting for transfers between devices  20 us (13%)
  local copies, waits for them, and re-layouts  1.81 us (1%)
    all_to_all x2, blocking collectives, exchange(): return lax.all_to_all(array, axes, split_axis=0, concat_axis=0, tiled=True)  58.5 us
    all_to_all x2, starting transfers between devices, exchange(): return lax.all_to_all(array, axes, split_axis=0, concat_axis=0, tiled=True)  32.5 us
    all_to_all x2, waiting for transfers between devices, exchange(): return lax.all_to_all(array, axes, split_axis=0, concat_axis=0, tiled=True)  16.1 us
    pallas_call x1, Pallas kernels, mixer(): call(backward_kernel, STEPS, [pl.BlockSpec((size, T + 8, 768), back), pl....  15.6 us
    pallas_call x1, Pallas kernels, mixer(): call(forward_kernel, STEPS, [pl.BlockSpec((size, T + 8, 768), along), who...  13.5 us
    pallas_call x1, Pallas kernels, mixer(): call(gain_kernel, D // GAIN_BLOCKS, [pl.BlockSpec((GAIN_BLOCKS, T, 512),...  4.96 us
    ppermute x2, starting transfers between devices, mixer(): parts = parts + lax.ppermute(parts, axis, [(0, 1), (1, 0)])  4.68 us
    ppermute x2, waiting for transfers between devices, mixer(): parts = parts + lax.ppermute(parts, axis, [(0, 1), (1, 0)])  3.82 us
  transfers between devices with their start and end apart: 4, of which 4 were waited for; matrix products, arithmetic and copies ran while one was open for 1% of the time, Pallas kernels for 10%

profile of v2, /device:TPU:2, one launch (start us, length us, event | category | flops | bytes accessed | tf_op | source)
XLA Modules:
  0.0 158.5 jit_solution(7507179055575871219)
XLA Ops:
  0.6 3.1 %shard_map.111 = bf16[16,136,768]{2,1,0:T(8,128)(2,1)} custom-call(bf16[128,4096]{1,0:T(8,128)(2,1)} %bitcast.14, bf16[128,4096]{1,0:T(8,128)(2,1)} %bitcast.15, bf16[128,512]{1,0:T(8,128)(2,1)} %bitcast.16, bf16[128,512]{1,0:T(8,128)(2,1)} %bitcast.17, s32[64,128]{1,0:T(8,128)} %bitcast.18, s32[64,128]{1,0:T(8,128)} %bitcast.19), custom_call_target="tpu_custom_call" | custom-call | bytes 1048576 | tf_op jit(solution)/shard_map/pallas_call | solution.py:322
  3.8 49.2 %all_to_all.20.in_ref = bf16[16,136,768]{2,1,0:T(8,128)(2,1)} all-to-all(bf16[16,136,768]{2,1,0:T(8,128)(2,1)} %shard_map.111), channel_id=1, replica_groups=mesh['seq_0'=4,'seq_1'=4,'z_high'=16,'z_low'=2,'core'=2] {'seq_0','seq_1'}, dimensions={0} | all-to-all | bytes 6684672 | tf_op jit(solution)/shard_map/all_to_all | solution.py:318
  53.0 13.5 %shard_map.112 = (f32[16,128,256]{2,1,0:T(8,128)}, bf16[16,128,256]{2,1,0:T(8,128)(2,1)}, f32[4,32,128]{2,1,0:T(8,128)}) custom-call(bf16[16,136,768]{2,1,0:T(8,128)(2,1)} %all_to_all.20.in_ref, f32[1,256]{1,0:T(1,128)} %bitcast.20, f32[4]{0:T(128)} %skip_ref.3), custom_call_target="tpu_custom_call" | custom-call | bytes 1048576 | tf_op jit(solution)/shard_map/pallas_call | solution.py:348
  66.6 9.2 %all_to_all.21.stats_ref = f32[4,32,128]{2,1,0:T(8,128)} all-to-all(f32[4,32,128]{2,1,0:T(8,128)} %get-tuple-element.11), channel_id=1, replica_groups=mesh['seq_0'=4,'seq_1'=4,'z_high'=16,'z_low'=2,'core'=2] {'seq_1'}, dimensions={0} | all-to-all | bytes 131072 | tf_op jit(solution)/shard_map/all_to_all | solution.py:318
  75.8 5.0 %shard_map.115 = f32[16,2,256]{2,1,0:T(2,128)} custom-call(bf16[16,136,768]{2,1,0:T(8,128)(2,1)} %all_to_all.20.in_ref, f32[16,128,256]{2,1,0:T(8,128)} %get-tuple-element.9.mo_ref, f32[4,32,128]{2,1,0:T(8,128)} %all_to_all.21.stats_ref, f32[1,256]{1,0:T(1,128)} %bitcast.21), custom_call_target="tpu_custom_call" | custom-call | bytes 1048576 | tf_op jit(solution)/shard_map/pallas_call | solution.py:368
  80.7 27.5 %all-to-all-start.3 = ((f32[16,2,256]{2,1,0:T(2,128)}), f32[16,2,256]{2,1,0:T(2,128)S(1)}, u32[]{:S(2)}, u32[]{:S(2)}) async-start(f32[16,2,256]{2,1,0:T(2,128)} %shard_map.115), calls=%async_computation.3 | async-start | bytes 65536 | tf_op jit(solution)/shard_map/all_to_all | solution.py:318
  108.3 15.6 %shard_map.113 = bf16[16,128,384]{2,1,0:T(8,128)(2,1)} custom-call(bf16[16,136,768]{2,1,0:T(8,128)(2,1)} %all_to_all.20.in_ref, f32[16,128,256]{2,1,0:T(8,128)} %get-tuple-element.9.mo_ref, bf16[16,128,256]{2,1,0:T(8,128)(2,1)} %get-tuple-element.10.carried_ref, f32[4,32,128]{2,1,0:T(8,128)} %all_to_all.21.stats_ref, f32[1,256]{1,0:T(1,128)} %bitcast.22, ...), custom_call_target="tpu_custom_call" | custom-call | flops 17179869184 | bytes 1048576 | tf_op jit(solution)/shard_map/pallas_call | solution.py:384
  123.9 6.7 %all-to-all-done.3 = f32[16,2,256]{2,1,0:T(2,128)S(1)} async-done(((f32[16,2,256]{2,1,0:T(2,128)}), f32[16,2,256]{2,1,0:T(2,128)S(1)}, u32[]{:S(2)}, u32[]{:S(2)}) %all-to-all-start.3) | async-done | bytes 32800 | tf_op jit(solution)/shard_map/all_to_all | solution.py:318
  130.6 5.0 %all-to-all-start.2 = ((bf16[16,128,384]{2,1,0:T(8,128)(2,1)}), bf16[16,128,384]{2,1,0:T(8,128)(2,1)S(1)}, u32[]{:S(2)}, u32[]{:S(2)}) async-start(bf16[16,128,384]{2,1,0:T(8,128)(2,1)} %shard_map.113), calls=%async_computation.2 | async-start | bytes 3145728 | tf_op jit(solution)/shard_map/all_to_all | solution.py:318
  135.6 1.9 %collective-permute-start = (f32[2,256]{1,0:T(2,128)S(1)}, f32[2,256]{1,0:T(2,128)S(1)}, u32[]{:S(2)}, u32[]{:S(2)}) collective-permute-start(f32[2,256]{1,0:T(2,128)S(1)} %reduce_sum.18), channel_id=1, source_target_pairs={{0,1},{1,0},{2,3},{3,2},{4,5},{5,4},{6,7},{7,6},{8,9},{9,8},{10,11... | collective-permute-start | bytes 6152 | tf_op jit(solution)/shard_map/ppermute | solution.py:405
  137.5 1.1 collective-permute-done
  138.6 2.8 %collective-permute-start.1 = (f32[2,256]{1,0:T(2,128)S(1)}, f32[2,256]{1,0:T(2,128)S(1)}, u32[]{:S(2)}, u32[]{:S(2)}) collective-permute-start(f32[2,256]{1,0:T(2,128)S(1)} %add.6), channel_id=1, source_target_pairs={{0,2},{2,0},{1,3},{3,1},{4,6},{6,4},{5,7},{7,5},{8,10},{10,8},{9,1... | collective-permute-start | bytes 6152 | tf_op jit(solution)/shard_map/ppermute | solution.py:405
  141.4 2.7 %collective-permute-done.1 = f32[2,256]{1,0:T(2,128)S(1)} collective-permute-done((f32[2,256]{1,0:T(2,128)S(1)}, f32[2,256]{1,0:T(2,128)S(1)}, u32[]{:S(2)}, u32[]{:S(2)}) %collective-permute-start.1) | collective-permute-done | bytes 2080 | tf_op jit(solution)/shard_map/ppermute | solution.py:405
  144.1 0.6 slice_reduce_fusion
  144.6 0.1 reshape_squeeze.3
  144.7 0.6 reduce_sum.19
  145.4 9.4 %all-to-all-done.2.in_ref = bf16[16,128,384]{2,1,0:T(8,128)(2,1)S(1)} async-done(((bf16[16,128,384]{2,1,0:T(8,128)(2,1)}), bf16[16,128,384]{2,1,0:T(8,128)(2,1)S(1)}, u32[]{:S(2)}, u32[]{:S(2)}) %all-to-all-start.2) | async-done | bytes 1572896 | tf_op jit(solution)/shard_map/all_to_all | solution.py:318
  154.8 0.0 copy-start
  154.8 1.2 copy-done
  156.0 2.5 %shard_map.114 = (bf16[128,4096]{1,0:T(8,128)(2,1)}, bf16[128,512]{1,0:T(8,128)(2,1)}) custom-call(bf16[16,128,384]{2,1,0:T(8,128)(2,1)} %copy-done), custom_call_target="tpu_custom_call" | custom-call | tf_op jit(solution)/shard_map/pallas_call | solution.py:406
  (3 shorter events, 0.0 us)
Async XLA Ops:
  80.7 49.8 %all-to-all-start.3 = ((f32[16,2,256]{2,1,0:T(2,128)}), f32[16,2,256]{2,1,0:T(2,128)S(1)}, u32[]{:S(2)}, u32[]{:S(2)}) async-start(f32[16,2,256]{2,1,0:T(2,128)} %shard_map.115), calls=%async_computation.3 | async-start | bytes 65536 | tf_op jit(solution)/shard_map/all_to_all | solution.py:318
  130.6 24.2 %all-to-all-start.2 = ((bf16[16,128,384]{2,1,0:T(8,128)(2,1)}), bf16[16,128,384]{2,1,0:T(8,128)(2,1)S(1)}, u32[]{:S(2)}, u32[]{:S(2)}) async-start(bf16[16,128,384]{2,1,0:T(8,128)(2,1)} %shard_map.113), calls=%async_computation.2 | async-start | bytes 3145728 | tf_op jit(solution)/shard_map/all_to_all | solution.py:318
  135.6 3.0 %collective-permute-start = (f32[2,256]{1,0:T(2,128)S(1)}, f32[2,256]{1,0:T(2,128)S(1)}, u32[]{:S(2)}, u32[]{:S(2)}) collective-permute-start(f32[2,256]{1,0:T(2,128)S(1)} %reduce_sum.18), channel_id=1, source_target_pairs={{0,1},{1,0},{2,3},{3,2},{4,5},{5,4},{6,7},{7,6},{8,9},{9,8},{10,11... | collective-permute-start | bytes 6152 | tf_op jit(solution)/shard_map/ppermute | solution.py:405
  138.6 5.5 %collective-permute-start.1 = (f32[2,256]{1,0:T(2,128)S(1)}, f32[2,256]{1,0:T(2,128)S(1)}, u32[]{:S(2)}, u32[]{:S(2)}) collective-permute-start(f32[2,256]{1,0:T(2,128)S(1)} %add.6), channel_id=1, source_target_pairs={{0,2},{2,0},{1,3},{3,1},{4,6},{6,4},{5,7},{7,5},{8,10},{10,8},{9,1... | collective-permute-start | bytes 6152 | tf_op jit(solution)/shard_map/ppermute | solution.py:405
  154.8 1.2 copy-start

commit v3 on v2

--- a/solution.py
+++ b/solution.py
@@ -19,11 +19,12 @@
 SEQ = ("seq_0", "seq_1")
 F32 = jnp.float32
 BF16 = jnp.bfloat16
-BLOCKS_PER_STEP = 2
+BLOCKS_PER_STEP = 4
 STEPS = D // BLOCKS_PER_STEP
 PACK_STEPS = 2
-GAIN_BLOCKS = 4
+GAIN_BLOCKS = 8
 FAR = -1e30
+X_AT, UP_AT, WRITE_AT, READ_AT, TAIL_AT, ROWS = 0, 256, 512, 640, 768, 784
 
 
 def contract(left, right, dims):
@@ -35,37 +36,85 @@
     high = (dec >> 8).astype(F32)
     low = (dec & 255).astype(F32)
     steps = dt_ref[...].astype(F32)
+    top = lax.broadcasted_iota(jnp.int32, (8, 128), 0) < HEADS
     for j in range(D // PACK_STEPS):
-        cols = slice(LANES * j, LANES * (j + 1))
         group = slice(N * (j // 4), N * (j // 4 + 1))
-        out_ref[j, :T, :256] = x_ref[:, cols]
-        out_ref[j, :T, 256:512] = up_ref[:, cols]
-        out_ref[j, :T, 512:640] = write_ref[:, group]
-        out_ref[j, :T, 640:768] = read_ref[:, group]
+        for half in range(2):
+            cols = slice(LANES * j + 128 * half, LANES * j + 128 * (half + 1))
+            out_ref[j, X_AT + T * half : X_AT + T * (half + 1)] = x_ref[:, cols]
+            out_ref[j, UP_AT + T * half : UP_AT + T * (half + 1)] = up_ref[:, cols]
+        out_ref[j, WRITE_AT : WRITE_AT + T] = write_ref[:, group]
+        out_ref[j, READ_AT : READ_AT + T] = read_ref[:, group]
         base = 8 * (j // 2)
-        for place, rows in enumerate((steps, high, low)):
-            eight = rows[base : base + 8]
-            if j % 2 == 1:
-                eight = pltpu.roll(eight, 4, 0)
-            out_ref[j, T:, 128 * place : 128 * (place + 1)] = eight.astype(BF16)
-        out_ref[j, T:, 384:] = jnp.zeros((8, 384), BF16)
-
-
-def scalars(tail):
+        steps8, high8, low8 = (rows[base : base + 8] for rows in (steps, high, low))
+        if j % 2 == 1:
+            steps8, low8 = pltpu.roll(steps8, HEADS, 0), pltpu.roll(low8, HEADS, 0)
+        else:
+            high8 = pltpu.roll(high8, HEADS, 0)
+        tail = jnp.concatenate([jnp.where(top, steps8, high8), low8], axis=0)
+        out_ref[j, TAIL_AT:ROWS] = tail.astype(BF16)
+
+
+def wide(ref, b, at):
+    return jnp.concatenate([ref[b, at : at + T], ref[b, at + T : at + 2 * T]], axis=1).astype(F32)
+
+
+def rows_of(tail):
     upto = (
         lax.broadcasted_iota(jnp.int32, (T, T), 0) <= lax.broadcasted_iota(jnp.int32, (T, T), 1)
     ).astype(F32).astype(BF16)
-    step = tail[:, :128].astype(F32) / 16.0
-    whole = contract(tail[:, 128:256], upto, ((1,), (0,))) * 256.0 + contract(
-        tail[:, 256:384], upto, ((1,), (0,))
+    tail = tail.astype(F32)
+    step = tail[:8] / 16.0
+    high = pltpu.roll(tail[:8], HEADS, 0).astype(BF16)
+    whole = contract(high, upto, ((1,), (0,))) * 256.0 + contract(
+        tail[8:].astype(BF16), upto, ((1,), (0,))
     )
     log_decay = -(whole / 65536.0)
     last = jnp.broadcast_to(log_decay[:, T - 1 : T], (8, T))
     ending = jnp.exp(last - log_decay) * step
     readout = jnp.exp(log_decay)
     block_decay = jnp.exp(last).astype(BF16).astype(F32)
+    return log_decay, step, block_decay, ending, readout
+
+
+def scalars(tail):
+    log_decay, step, block_decay, ending, readout = rows_of(tail)
     cols = jnp.transpose(jnp.concatenate([log_decay, step, ending, readout], axis=0))
     return log_decay, step, block_decay, cols
+
+
+def thirds(rows):
+    high = rows.astype(BF16).astype(F32)
+    middle = (rows - high).astype(BF16).astype(F32)
+    return high, middle, rows - high - middle
+
+
+def head_marks(rows, width):
+    row = lax.broadcasted_iota(jnp.int32, (rows, HEADS * width), 0) % 8
+    lane = lax.broadcasted_iota(jnp.int32, (rows, HEADS * width), 1) // width
+    return (row == lane).astype(F32)
+
+
+def gaps(log_decay, marks):
+    parts = thirds(log_decay)
+    place = lax.broadcasted_iota(jnp.int32, (8, T), 0)
+    minus = []
+    for j in range(HEADS):
+        tile = jnp.zeros((8, T), F32)
+        for n, part in enumerate(parts):
+            tile = jnp.where(place == n, -part[j : j + 1], tile)
+        minus.append(tile)
+    left = jnp.concatenate([*parts, jnp.ones((8, T), F32)], axis=0).astype(BF16)
+    right = jnp.concatenate([marks, jnp.concatenate(minus, axis=1)], axis=0).astype(BF16)
+    return contract(left, right, ((0,), (0,)))
+
+
+def spread_two(ending, readout, marks):
+    both = []
+    for rows in (ending, readout):
+        left = jnp.concatenate(thirds(rows), axis=0).astype(BF16)
+        both.append(contract(left, marks, ((0,), (0,))))
+    return both
 
 
 def low_half(shape):
@@ -121,22 +170,26 @@
     row_id = lax.broadcasted_iota(jnp.int32, (T, T), 0)
     lane_id = lax.broadcasted_iota(jnp.int32, (T, T), 1)
     causal = row_id >= lane_id
+    marks = head_marks(24, P_SIZE).astype(BF16)
+    wide_marks = head_marks(24, T)
     state = carry[...]
     found = sums[...]
     results = []
     for b in range(BLOCKS_PER_STEP):
-        x = in_ref[b, :T, :256].astype(F32)
-        up = in_ref[b, :T, 256:512].astype(F32)
-        write = in_ref[b, :T, 512:640]
-        read = in_ref[b, :T, 640:768]
-        log_decay, step, block_decay, cols = scalars(in_ref[b, T:, :])
+        x = wide(in_ref, b, X_AT)
+        up = wide(in_ref, b, UP_AT)
+        write = in_ref[b, WRITE_AT : WRITE_AT + T]
+        read = in_ref[b, READ_AT : READ_AT + T]
+        log_decay, step, block_decay, ending, readout = rows_of(in_ref[b, TAIL_AT:])
+        gap = gaps(log_decay, wide_marks)
+        ending, readout = spread_two(ending, readout, marks)
         scores = contract(read, write, ((1,), (1,)))
         inner = []
         for i in range(HEADS // 2):
             mixing = []
             for j in (2 * i, 2 * i + 1):
-                gap = jnp.where(causal, cols[:, j : j + 1] - log_decay[j : j + 1], FAR)
-                mixing.append((scores * (jnp.exp(gap) * step[j : j + 1])).astype(BF16))
+                decay = jnp.exp(jnp.where(causal, gap[:, T * j : T * (j + 1)], FAR))
+                mixing.append((scores * (decay * step[j : j + 1])).astype(BF16))
             inner.append(
                 contract(
                     jnp.concatenate(mixing, axis=1),
@@ -144,19 +197,19 @@
                     ((1,), (0,)),
                 )
             )
-        weighted = (x * spread(cols, 16)).astype(BF16)
+        weighted = (x * ending).astype(BF16)
         span_state = contract(write, weighted, ((0,), (0,))).astype(BF16).astype(F32)
         carried = state.astype(BF16)
         state = (spread_rows(block_decay) * state + span_state).astype(BF16).astype(F32)
         out = (
             jnp.concatenate(inner, axis=1)
-            + spread(cols, 24) * contract(read, carried, ((1,), (0,)))
+            + readout * contract(read, carried, ((1,), (0,)))
             + skip * x
         )
         square = jnp.sum(out * out, axis=1, keepdims=True)
         cross = jnp.sum(up * gain * out, axis=1, keepdims=True)
-        at = 2 * (BLOCKS_PER_STEP * step_id + b)
-        found = jnp.where(lane_id == at, square, jnp.where(lane_id == at + 1, cross, found))
+        at = BLOCKS_PER_STEP * step_id + b
+        found = jnp.where(lane_id == at, square, jnp.where(lane_id == D + at, cross, found))
         results.append((out, carried))
     for b, (out, carried) in enumerate(results):
         mo_ref[b] = out
@@ -171,15 +224,23 @@
             stats_ref[d] = rows
 
 
-def shared_sums(stats_ref):
+def shared_sums(stats_ref, sums):
     total = stats_ref[0] + stats_ref[1] + stats_ref[2] + stats_ref[3]
-    return jnp.transpose(jnp.concatenate([total] * 4, axis=0))
-
-
-def normalise(found, block, out, up, gain):
-    here = pltpu.roll(found, lax.rem(128 - 2 * block, 128), 1)
-    inverse = lax.rsqrt(here[:, 0:1] / (HG * P_SIZE) + 1e-05)
-    mean = inverse * here[:, 1:2] / (HG * P_SIZE)
+    inverse = lax.rsqrt(total[:D] / (HG * P_SIZE) + 1e-05)
+    mean = inverse * total[D:] / (HG * P_SIZE)
+    for n, part in enumerate((*thirds(inverse), *thirds(mean))):
+        sums[n] = part
+
+
+def normalise(sums, block, out, up, gain):
+    place = lax.broadcasted_iota(jnp.int32, (8, T), 0)
+    rows = jnp.zeros((8, T), F32)
+    for n in range(6):
+        rows = jnp.where(place == n, sums[n, pl.ds(block, 1), :], rows)
+    row = lax.broadcasted_iota(jnp.int32, (8, 2 * LANES), 0) // 3
+    lane = lax.broadcasted_iota(jnp.int32, (8, 2 * LANES), 1) // LANES
+    both = contract(rows.astype(BF16), (row == lane).astype(F32).astype(BF16), ((0,), (0,)))
+    inverse, mean = both[:, :LANES], both[:, LANES:]
     normed = out * inverse
     return normed, inverse * (up * gain - normed * mean)
 
@@ -190,16 +251,15 @@
     @pl.when(step_id == 0)
     def _():
         parts[...] = jnp.zeros_like(parts)
-        sums[...] = shared_sums(stats_ref)
+        shared_sums(stats_ref, sums)
 
     gain = gain_ref[...]
-    found = sums[...]
     gain_sum = parts[0]
     skip_sum = parts[1]
     for b in range(GAIN_BLOCKS):
-        x = in_ref[b, :, :256].astype(F32)
-        up = in_ref[b, :, 256:].astype(F32)
-        normed, delta = normalise(found, GAIN_BLOCKS * step_id + b, mo_ref[b], up, gain)
+        x = wide(in_ref, b, X_AT)
+        up = wide(in_ref, b, UP_AT)
+        normed, delta = normalise(sums, GAIN_BLOCKS * step_id + b, mo_ref[b], up, gain)
         gain_sum = gain_sum + jnp.sum((up * normed).reshape(T // 8, 8, LANES), axis=0)
         skip_sum = skip_sum + jnp.sum((delta * x).reshape(T // 8, 8, LANES), axis=0)
     parts[0] = gain_sum
@@ -223,7 +283,7 @@
     @pl.when(step_id == 0)
     def _():
         carry[...] = jnp.zeros_like(carry)
-        sums[...] = shared_sums(stats_ref)
+        shared_sums(stats_ref, sums)
 
     gain = gain_ref[...]
     skip = skip_lanes(skip_ref)
@@ -233,15 +293,14 @@
     state = carry[...]
     results = []
     first = BLOCKS_PER_STEP * (STEPS - 1 - step_id)
-    found = sums[...]
     for b in reversed(range(BLOCKS_PER_STEP)):
-        x = in_ref[b, :T, :256].astype(F32)
-        up = in_ref[b, :T, 256:512].astype(F32)
-        write = in_ref[b, :T, 512:640]
-        read = in_ref[b, :T, 640:768]
+        x = wide(in_ref, b, X_AT)
+        up = wide(in_ref, b, UP_AT)
+        write = in_ref[b, WRITE_AT : WRITE_AT + T]
+        read = in_ref[b, READ_AT : READ_AT + T]
         out = mo_ref[b]
-        log_decay, _, block_decay, cols = scalars(in_ref[b, T:, :])
-        _, delta = normalise(found, first + b, out, up, gain)
+        log_decay, _, block_decay, cols = scalars(in_ref[b, TAIL_AT:])
+        _, delta = normalise(sums, first + b, out, up, gain)
         scaled = (delta * spread(cols, 24)).astype(BF16)
         half = delta.astype(BF16)
         scores = contract(write, read, ((1,), (1,)))
@@ -274,8 +333,10 @@
         state = (state_grad + spread_rows(block_decay) * state).astype(BF16).astype(F32)
         results.append((b, mixer_grad, read_grad))
     for b, mixer_grad, read_grad in results:
-        out_ref[b, :, :256] = mixer_grad.astype(BF16)
-        out_ref[b, :, 256:] = read_grad.astype(BF16)
+        mixer_grad = mixer_grad.astype(BF16)
+        out_ref[b, :T] = mixer_grad[:, :128]
+        out_ref[b, T : 2 * T] = mixer_grad[:, 128:]
+        out_ref[b, 2 * T :] = read_grad.astype(BF16)
     carry[...] = state
 
 
@@ -283,8 +344,10 @@
     for g in range(G):
         total = jnp.zeros((T, N), F32)
         for d in range(4 * g, 4 * g + 4):
-            mixer_ref[:, LANES * d : LANES * (d + 1)] = in_ref[d, :, :256]
-            total = total + in_ref[d, :, 256:].astype(F32)
+            for half in range(2):
+                at = LANES * d + 128 * half
+                mixer_ref[:, at : at + 128] = in_ref[d, T * half : T * (half + 1)]
+            total = total + in_ref[d, 2 * T :].astype(F32)
         read_ref[:, N * g : N * (g + 1)] = total.astype(BF16)
 
 
@@ -330,8 +393,8 @@
                 pl.BlockSpec((H // PACK_STEPS, T), lambda i: (i, 0)),
                 pl.BlockSpec((H // PACK_STEPS, T), lambda i: (i, 0)),
             ],
-            pl.BlockSpec((D // PACK_STEPS, T + 8, 768), lambda i: (i, 0, 0)),
-            shape((D, T + 8, 768), BF16),
+            pl.BlockSpec((D // PACK_STEPS, ROWS, 128), lambda i: (i, 0, 0)),
+            shape((D, ROWS, 128), BF16),
             interpret=interpret,
         )(
             mixer_in[0],
@@ -348,7 +411,7 @@
         mixer_out, carried, stats = call(
             forward_kernel,
             STEPS,
-            [pl.BlockSpec((size, T + 8, 768), along), whole((1, LANES)), SCALARS],
+            [pl.BlockSpec((size, ROWS, 128), along), whole((1, LANES)), SCALARS],
             [
                 pl.BlockSpec((size, T, LANES), along),
                 pl.BlockSpec((size, N, LANES), along),
@@ -369,14 +432,14 @@
             gain_kernel,
             D // GAIN_BLOCKS,
             [
-                pl.BlockSpec((GAIN_BLOCKS, T, 512), along),
+                pl.BlockSpec((GAIN_BLOCKS, WRITE_AT, 128), along),
                 pl.BlockSpec((GAIN_BLOCKS, T, LANES), along),
                 whole((4, 2 * D, T)),
                 whole((1, LANES)),
             ],
             whole((far, 2, LANES)),
             shape((far, 2, LANES), F32),
-            [pltpu.VMEM((T, T), F32), pltpu.VMEM((2, 8, LANES), F32)],
+            [pltpu.VMEM((6, D, T), F32), pltpu.VMEM((2, 8, LANES), F32)],
             interpret=interpret,
         )(blocks, mixer_out, stats, gain)
         parts = exchange(copies, "z_high") if far > 1 else copies
@@ -385,16 +448,16 @@
             backward_kernel,
             STEPS,
             [
-                pl.BlockSpec((size, T + 8, 768), back),
+                pl.BlockSpec((size, ROWS, 128), back),
                 pl.BlockSpec((size, T, LANES), back),
                 pl.BlockSpec((size, N, LANES), back),
                 whole((4, 2 * D, T)),
                 whole((1, LANES)),
                 SCALARS,
             ],
-            pl.BlockSpec((size, T, 384), back),
-            shape((D, T, 384), BF16),
-            [pltpu.VMEM((N, LANES), F32), pltpu.VMEM((T, T), F32)],
+            pl.BlockSpec((size, 3 * T, 128), back),
+            shape((D, 3 * T, 128), BF16),
+            [pltpu.VMEM((N, LANES), F32), pltpu.VMEM((6, D, T), F32)],
             flops=1 << 34,
             interpret=interpret,
         )(blocks, mixer_out, carried, stats, gain, skip_gain)
@@ -405,7 +468,6 @@
                 parts = parts + lax.ppermute(parts, axis, [(0, 1), (1, 0)])
         mixer_grad, read_grad = pl.pallas_call(
             unpack_kernel,
-            in_specs=[pl.BlockSpec(memory_space=pltpu.VMEM)],
             out_shape=[shape((T, H * P_SIZE), BF16), shape((T, G * N), BF16)],
             interpret=interpret,
         )(grads)

time: 159 us -> 154 us (0.969)
  the two profiles are of different devices: /device:TPU:2 before, /device:TPU:32 now
where the time goes in v3:
time: 154 us
  blocking collectives  57.1 us (37%)
  starting transfers between devices  36.2 us (24%)
  Pallas kernels  35.5 us (23%)
  waiting for transfers between devices  21.7 us (14%)
  local copies, waits for them, and re-layouts  1.81 us (1%)
    all_to_all x2, blocking collectives, exchange(): return lax.all_to_all(array, axes, split_axis=0, concat_axis=0, tiled=True)  57.1 us
    all_to_all x2, starting transfers between devices, exchange(): return lax.all_to_all(array, axes, split_axis=0, concat_axis=0, tiled=True)  31.2 us
    all_to_all x2, waiting for transfers between devices, exchange(): return lax.all_to_all(array, axes, split_axis=0, concat_axis=0, tiled=True)  18.1 us
    pallas_call x1, Pallas kernels, mixer(): call(backward_kernel, STEPS, [pl.BlockSpec((size, ROWS, 128), back), pl.B...  14.7 us
    pallas_call x1, Pallas kernels, mixer(): call(forward_kernel, STEPS, [pl.BlockSpec((size, ROWS, 128), along), whol...  11.5 us
    ppermute x2, starting transfers between devices, mixer(): parts = parts + lax.ppermute(parts, axis, [(0, 1), (1, 0)])  4.95 us
    ppermute x2, waiting for transfers between devices, mixer(): parts = parts + lax.ppermute(parts, axis, [(0, 1), (1, 0)])  3.55 us
    pallas_call x1, Pallas kernels, mixer(): call(gain_kernel, D // GAIN_BLOCKS, [pl.BlockSpec((GAIN_BLOCKS, WRITE_AT,...  3.42 us
  transfers between devices with their start and end apart: 4, of which 4 were waited for; matrix products, arithmetic and copies ran while one was open for 1% of the time, Pallas kernels for 10%

profile of v3, /device:TPU:32, one launch (start us, length us, event | category | flops | bytes accessed | tf_op | source)
XLA Modules:
  0.0 153.7 jit_solution(12150072141011912649)
XLA Ops:
  0.6 3.2 %shard_map.111 = bf16[16,784,128]{2,1,0:T(8,128)(2,1)} custom-call(bf16[128,4096]{1,0:T(8,128)(2,1)} %bitcast.14, bf16[128,4096]{1,0:T(8,128)(2,1)} %bitcast.15, bf16[128,512]{1,0:T(8,128)(2,1)} %bitcast.16, bf16[128,512]{1,0:T(8,128)(2,1)} %bitcast.17, s32[64,128]{1,0:T(8,128)} %bitcast.18, s32[64,128]{1,0:T(8,128)} %bitcast.19), custom_call_target="tpu_custom_call" | custom-call | bytes 1048576 | tf_op jit(solution)/shard_map/pallas_call | solution.py:385
  3.8 47.5 %all_to_all.20.in_ref = bf16[16,784,128]{2,1,0:T(8,128)(2,1)} all-to-all(bf16[16,784,128]{2,1,0:T(8,128)(2,1)} %shard_map.111), channel_id=1, replica_groups=mesh['seq_0'=4,'seq_1'=4,'z_high'=16,'z_low'=2,'core'=2] {'seq_0','seq_1'}, dimensions={0} | all-to-all | bytes 6422528 | tf_op jit(solution)/shard_map/all_to_all | solution.py:381
  51.3 11.5 %shard_map.112 = (f32[16,128,256]{2,1,0:T(8,128)}, bf16[16,128,256]{2,1,0:T(8,128)(2,1)}, f32[4,32,128]{2,1,0:T(8,128)}) custom-call(bf16[16,784,128]{2,1,0:T(8,128)(2,1)} %all_to_all.20.in_ref, f32[1,256]{1,0:T(1,128)} %bitcast.20, f32[4]{0:T(128)} %skip_ref.3), custom_call_target="tpu_custom_call" | custom-call | bytes 1048576 | tf_op jit(solution)/shard_map/pallas_call | solution.py:411
  62.8 9.6 %all_to_all.21.stats_ref = f32[4,32,128]{2,1,0:T(8,128)} all-to-all(f32[4,32,128]{2,1,0:T(8,128)} %get-tuple-element.11), channel_id=1, replica_groups=mesh['seq_0'=4,'seq_1'=4,'z_high'=16,'z_low'=2,'core'=2] {'seq_1'}, dimensions={0} | all-to-all | bytes 131072 | tf_op jit(solution)/shard_map/all_to_all | solution.py:381
  72.4 3.4 %shard_map.115 = f32[16,2,256]{2,1,0:T(2,128)} custom-call(bf16[16,784,128]{2,1,0:T(8,128)(2,1)} %all_to_all.20.in_ref, f32[16,128,256]{2,1,0:T(8,128)} %get-tuple-element.9.mo_ref, f32[4,32,128]{2,1,0:T(8,128)} %all_to_all.21.stats_ref, f32[1,256]{1,0:T(1,128)} %bitcast.21), custom_call_target="tpu_custom_call" | custom-call | bytes 1048576 | tf_op jit(solution)/shard_map/pallas_call | solution.py:431
  75.9 27.5 %all-to-all-start.3 = ((f32[16,2,256]{2,1,0:T(2,128)}), f32[16,2,256]{2,1,0:T(2,128)S(1)}, u32[]{:S(2)}, u32[]{:S(2)}) async-start(f32[16,2,256]{2,1,0:T(2,128)} %shard_map.115), calls=%async_computation.3 | async-start | bytes 65536 | tf_op jit(solution)/shard_map/all_to_all | solution.py:381
  103.4 14.7 %shard_map.113 = bf16[16,384,128]{2,1,0:T(8,128)(2,1)} custom-call(bf16[16,784,128]{2,1,0:T(8,128)(2,1)} %all_to_all.20.in_ref, f32[16,128,256]{2,1,0:T(8,128)} %get-tuple-element.9.mo_ref, bf16[16,128,256]{2,1,0:T(8,128)(2,1)} %get-tuple-element.10.carried_ref, f32[4,32,128]{2,1,0:T(8,128)} %all_to_all.21.stats_ref, f32[1,256]{1,0:T(1,128)} %bitcast.22, ...), custom_call_target="tpu_custom_call" | custom-call | flops 17179869184 | bytes 1048576 | tf_op jit(solution)/shard_map/pallas_call | solution.py:447
  118.1 7.5 %all-to-all-done.3 = f32[16,2,256]{2,1,0:T(2,128)S(1)} async-done(((f32[16,2,256]{2,1,0:T(2,128)}), f32[16,2,256]{2,1,0:T(2,128)S(1)}, u32[]{:S(2)}, u32[]{:S(2)}) %all-to-all-start.3) | async-done | bytes 32800 | tf_op jit(solution)/shard_map/all_to_all | solution.py:381
  125.6 3.7 %all-to-all-start.2 = ((bf16[16,384,128]{2,1,0:T(8,128)(2,1)}), bf16[16,384,128]{2,1,0:T(8,128)(2,1)S(1)}, u32[]{:S(2)}, u32[]{:S(2)}) async-start(bf16[16,384,128]{2,1,0:T(8,128)(2,1)} %shard_map.113), calls=%async_computation.2 | async-start | bytes 3145728 | tf_op jit(solution)/shard_map/all_to_all | solution.py:381
  129.3 1.9 %collective-permute-start = (f32[2,256]{1,0:T(2,128)S(1)}, f32[2,256]{1,0:T(2,128)S(1)}, u32[]{:S(2)}, u32[]{:S(2)}) collective-permute-start(f32[2,256]{1,0:T(2,128)S(1)} %reduce_sum.18), channel_id=1, source_target_pairs={{0,1},{1,0},{2,3},{3,2},{4,5},{5,4},{6,7},{7,6},{8,9},{9,8},{10,11... | collective-permute-start | bytes 6152 | tf_op jit(solution)/shard_map/ppermute | solution.py:468
  131.2 1.1 collective-permute-done
  132.4 3.0 %collective-permute-start.1 = (f32[2,256]{1,0:T(2,128)S(1)}, f32[2,256]{1,0:T(2,128)S(1)}, u32[]{:S(2)}, u32[]{:S(2)}) collective-permute-start(f32[2,256]{1,0:T(2,128)S(1)} %add.6), channel_id=1, source_target_pairs={{0,2},{2,0},{1,3},{3,1},{4,6},{6,4},{5,7},{7,5},{8,10},{10,8},{9,1... | collective-permute-start | bytes 6152 | tf_op jit(solution)/shard_map/ppermute | solution.py:468
  135.4 2.4 %collective-permute-done.1 = f32[2,256]{1,0:T(2,128)S(1)} collective-permute-done((f32[2,256]{1,0:T(2,128)S(1)}, f32[2,256]{1,0:T(2,128)S(1)}, u32[]{:S(2)}, u32[]{:S(2)}) %collective-permute-start.1) | collective-permute-done | bytes 2080 | tf_op jit(solution)/shard_map/ppermute | solution.py:468
  137.8 0.6 slice_reduce_fusion
  138.4 0.1 reshape_squeeze.3
  138.5 0.6 reduce_sum.19
  139.1 10.7 %all-to-all-done.2.in_ref = bf16[16,384,128]{2,1,0:T(8,128)(2,1)S(1)} async-done(((bf16[16,384,128]{2,1,0:T(8,128)(2,1)}), bf16[16,384,128]{2,1,0:T(8,128)(2,1)S(1)}, u32[]{:S(2)}, u32[]{:S(2)}) %all-to-all-start.2) | async-done | bytes 1572896 | tf_op jit(solution)/shard_map/all_to_all | solution.py:381
  149.8 0.0 copy-start
  149.8 1.2 copy-done
  151.0 2.7 %shard_map.114 = (bf16[128,4096]{1,0:T(8,128)(2,1)}, bf16[128,512]{1,0:T(8,128)(2,1)}) custom-call(bf16[16,384,128]{2,1,0:T(8,128)(2,1)} %copy-done), custom_call_target="tpu_custom_call" | custom-call | tf_op jit(solution)/shard_map/pallas_call | solution.py:469
  (3 shorter events, 0.0 us)
Async XLA Ops:
  75.9 49.7 %all-to-all-start.3 = ((f32[16,2,256]{2,1,0:T(2,128)}), f32[16,2,256]{2,1,0:T(2,128)S(1)}, u32[]{:S(2)}, u32[]{:S(2)}) async-start(f32[16,2,256]{2,1,0:T(2,128)} %shard_map.115), calls=%async_computation.3 | async-start | bytes 65536 | tf_op jit(solution)/shard_map/all_to_all | solution.py:381
  125.6 24.2 %all-to-all-start.2 = ((bf16[16,384,128]{2,1,0:T(8,128)(2,1)}), bf16[16,384,128]{2,1,0:T(8,128)(2,1)S(1)}, u32[]{:S(2)}, u32[]{:S(2)}) async-start(bf16[16,384,128]{2,1,0:T(8,128)(2,1)} %shard_map.113), calls=%async_computation.2 | async-start | bytes 3145728 | tf_op jit(solution)/shard_map/all_to_all | solution.py:381
  129.3 3.1 %collective-permute-start = (f32[2,256]{1,0:T(2,128)S(1)}, f32[2,256]{1,0:T(2,128)S(1)}, u32[]{:S(2)}, u32[]{:S(2)}) collective-permute-start(f32[2,256]{1,0:T(2,128)S(1)} %reduce_sum.18), channel_id=1, source_target_pairs={{0,1},{1,0},{2,3},{3,2},{4,5},{5,4},{6,7},{7,6},{8,9},{9,8},{10,11... | collective-permute-start | bytes 6152 | tf_op jit(solution)/shard_map/ppermute | solution.py:468
  132.4 5.5 %collective-permute-start.1 = (f32[2,256]{1,0:T(2,128)S(1)}, f32[2,256]{1,0:T(2,128)S(1)}, u32[]{:S(2)}, u32[]{:S(2)}) collective-permute-start(f32[2,256]{1,0:T(2,128)S(1)} %add.6), channel_id=1, source_target_pairs={{0,2},{2,0},{1,3},{3,1},{4,6},{6,4},{5,7},{7,5},{8,10},{10,8},{9,1... | collective-permute-start | bytes 6152 | tf_op jit(solution)/shard_map/ppermute | solution.py:468
  149.8 1.2 copy-start

commit v4 on v3

--- a/solution.py
+++ b/solution.py
@@ -17,6 +17,7 @@
 HEADS = H // D
 LANES = HEADS * P_SIZE
 SEQ = ("seq_0", "seq_1")
+NEAR = ("z_low", "core")
 F32 = jnp.float32
 BF16 = jnp.bfloat16
 BLOCKS_PER_STEP = 4
@@ -427,7 +428,7 @@
         )(blocks, gain, skip_gain)
         stats = exchange(stats, "seq_1")
 
-        far = lax.axis_size("z_high")
+        near = lax.axis_size(NEAR)
         copies = call(
             gain_kernel,
             D // GAIN_BLOCKS,
@@ -437,12 +438,12 @@
                 whole((4, 2 * D, T)),
                 whole((1, LANES)),
             ],
-            whole((far, 2, LANES)),
-            shape((far, 2, LANES), F32),
+            whole((near, 2, LANES)),
+            shape((near, 2, LANES), F32),
             [pltpu.VMEM((6, D, T), F32), pltpu.VMEM((2, 8, LANES), F32)],
             interpret=interpret,
         )(blocks, mixer_out, stats, gain)
-        parts = exchange(copies, "z_high") if far > 1 else copies
+        parts = exchange(copies, NEAR) if near > 1 else copies
         back = lambda i: (STEPS - 1 - i, 0, 0)
         grads = call(
             backward_kernel,
@@ -463,9 +464,11 @@
         )(blocks, mixer_out, carried, stats, gain, skip_gain)
         grads = exchange(grads, SEQ)
         parts = jnp.sum(parts, axis=0)
-        for axis in ("core", "z_low"):
-            if lax.axis_size(axis) == 2:
-                parts = parts + lax.ppermute(parts, axis, [(0, 1), (1, 0)])
+        if lax.axis_size("z_high") == 4:
+            one, two, three = (
+                lax.ppermute(parts, "z_high", [(i, i ^ d) for i in range(4)]) for d in (1, 2, 3)
+            )
+            parts = (parts + one) + (two + three)
         mixer_grad, read_grad = pl.pallas_call(
             unpack_kernel,
             out_shape=[shape((T, H * P_SIZE), BF16), shape((T, G * N), BF16)],
@@ -495,5 +498,5 @@
 
 def solution(mesh):
     names = ("seq_0", "seq_1", "z_high", "z_low", "core")
-    step = sharded(Mesh(mesh.devices.reshape(4, 4, 16, 2, 2), names))
+    step = sharded(Mesh(mesh.devices.reshape(4, 4, 4, 8, 2), names))
     return step

time: 154 us -> 155 us (level)
  the two profiles are of different devices: /device:TPU:32 before, /device:TPU:1 now
where the time goes in v4:
time: 155 us; the launch traced here: 154 us
  starting transfers between devices  57.3 us (37%)
  blocking collectives  46.7 us (30%)
  Pallas kernels  35.5 us (23%)
  waiting for transfers between devices  10.9 us (7%)
  local copies, waits for them, and re-layouts  1.82 us (1%)
    all_to_all x2, blocking collectives, exchange(): return lax.all_to_all(array, axes, split_axis=0, concat_axis=0, tiled=True)  46.7 us
    ppermute x3, starting transfers between devices, mixer(): lax.ppermute(parts, 'z_high', [(i, i ^ d) for i in range(4)])  29.2 us
    all_to_all x2, starting transfers between devices, exchange(): return lax.all_to_all(array, axes, split_axis=0, concat_axis=0, tiled=True)  28.1 us
    pallas_call x1, Pallas kernels, mixer(): call(backward_kernel, STEPS, [pl.BlockSpec((size, ROWS, 128), back), pl.B...  14.7 us
    pallas_call x1, Pallas kernels, mixer(): call(forward_kernel, STEPS, [pl.BlockSpec((size, ROWS, 128), along), whol...  11.5 us
    ppermute x3, waiting for transfers between devices, mixer(): lax.ppermute(parts, 'z_high', [(i, i ^ d) for i in range(4)])  10.9 us
    pallas_call x1, Pallas kernels, mixer(): call(gain_kernel, D // GAIN_BLOCKS, [pl.BlockSpec((GAIN_BLOCKS, WRITE_AT,...  3.43 us
    pallas_call x1, Pallas kernels, mixer(): call(pack_kernel, PACK_STEPS, [pl.BlockSpec((T, H * P_SIZE // PACK_STEPS)...  3.2 us
  transfers between devices with their start and end apart: 5, of which 2 were waited for; matrix products, arithmetic and copies ran while one was open for 1% of the time, Pallas kernels for 10%

profile of v4, /device:TPU:1, one launch (start us, length us, event | category | flops | bytes accessed | tf_op | source)
XLA Modules:
  0.0 153.6 jit_solution(671851207060380336)
XLA Ops:
  0.6 3.2 %shard_map.111 = bf16[16,784,128]{2,1,0:T(8,128)(2,1)} custom-call(bf16[128,4096]{1,0:T(8,128)(2,1)} %bitcast.14, bf16[128,4096]{1,0:T(8,128)(2,1)} %bitcast.15, bf16[128,512]{1,0:T(8,128)(2,1)} %bitcast.16, bf16[128,512]{1,0:T(8,128)(2,1)} %bitcast.17, s32[64,128]{1,0:T(8,128)} %bitcast.18, s32[64,128]{1,0:T(8,128)} %bitcast.19), custom_call_target="tpu_custom_call" | custom-call | bytes 1048576 | tf_op jit(solution)/shard_map/pallas_call | solution.py:386
  3.8 38.3 %all_to_all.20.in_ref = bf16[16,784,128]{2,1,0:T(8,128)(2,1)} all-to-all(bf16[16,784,128]{2,1,0:T(8,128)(2,1)} %shard_map.111), channel_id=1, replica_groups=mesh['seq_0'=4,'seq_1'=4,'z_high'=4,'z_low'=8,'core'=2] {'seq_0','seq_1'}, dimensions={0} | all-to-all | bytes 6422528 | tf_op jit(solution)/shard_map/all_to_all | solution.py:382
  42.1 11.5 %shard_map.112 = (f32[16,128,256]{2,1,0:T(8,128)}, bf16[16,128,256]{2,1,0:T(8,128)(2,1)}, f32[4,32,128]{2,1,0:T(8,128)}) custom-call(bf16[16,784,128]{2,1,0:T(8,128)(2,1)} %all_to_all.20.in_ref, f32[1,256]{1,0:T(1,128)} %bitcast.20, f32[4]{0:T(128)} %skip_ref.3), custom_call_target="tpu_custom_call" | custom-call | bytes 1048576 | tf_op jit(solution)/shard_map/pallas_call | solution.py:412
  53.6 8.4 %all_to_all.21.stats_ref = f32[4,32,128]{2,1,0:T(8,128)} all-to-all(f32[4,32,128]{2,1,0:T(8,128)} %get-tuple-element.11), channel_id=1, replica_groups=mesh['seq_0'=4,'seq_1'=4,'z_high'=4,'z_low'=8,'core'=2] {'seq_1'}, dimensions={0} | all-to-all | bytes 131072 | tf_op jit(solution)/shard_map/all_to_all | solution.py:382
  62.0 3.4 %shard_map.115 = f32[16,2,256]{2,1,0:T(2,128)} custom-call(bf16[16,784,128]{2,1,0:T(8,128)(2,1)} %all_to_all.20.in_ref, f32[16,128,256]{2,1,0:T(8,128)} %get-tuple-element.9.mo_ref, f32[4,32,128]{2,1,0:T(8,128)} %all_to_all.21.stats_ref, f32[1,256]{1,0:T(1,128)} %bitcast.21), custom_call_target="tpu_custom_call" | custom-call | bytes 1048576 | tf_op jit(solution)/shard_map/pallas_call | solution.py:432
  65.5 24.4 %all-to-all-start.3 = ((f32[16,2,256]{2,1,0:T(2,128)}), f32[16,2,256]{2,1,0:T(2,128)S(1)}, u32[]{:S(2)}, u32[]{:S(2)}) async-start(f32[16,2,256]{2,1,0:T(2,128)} %shard_map.115), calls=%async_computation.3 | async-start | bytes 65536 | tf_op jit(solution)/shard_map/all_to_all | solution.py:382
  89.9 14.7 %shard_map.113 = bf16[16,384,128]{2,1,0:T(8,128)(2,1)} custom-call(bf16[16,784,128]{2,1,0:T(8,128)(2,1)} %all_to_all.20.in_ref, f32[16,128,256]{2,1,0:T(8,128)} %get-tuple-element.9.mo_ref, bf16[16,128,256]{2,1,0:T(8,128)(2,1)} %get-tuple-element.10.carried_ref, f32[4,32,128]{2,1,0:T(8,128)} %all_to_all.21.stats_ref, f32[1,256]{1,0:T(1,128)} %bitcast.22, ...), custom_call_target="tpu_custom_call" | custom-call | flops 17179869184 | bytes 1048576 | tf_op jit(solution)/shard_map/pallas_call | solution.py:448
  104.6 0.0 all-to-all-done.3
  104.6 3.7 %all-to-all-start.2 = ((bf16[16,384,128]{2,1,0:T(8,128)(2,1)}), bf16[16,384,128]{2,1,0:T(8,128)(2,1)S(1)}, u32[]{:S(2)}, u32[]{:S(2)}) async-start(bf16[16,384,128]{2,1,0:T(8,128)(2,1)} %shard_map.113), calls=%async_computation.2 | async-start | bytes 3145728 | tf_op jit(solution)/shard_map/all_to_all | solution.py:382
  108.3 15.4 %collective-permute-start = (f32[2,256]{1,0:T(2,128)S(1)}, f32[2,256]{1,0:T(2,128)S(1)}, u32[]{:S(2)}, u32[]{:S(2)}) collective-permute-start(f32[2,256]{1,0:T(2,128)S(1)} %reduce_sum.18), channel_id=1, source_target_pairs={{0,16},{16,0},{32,48},{48,32},{1,17},{17,1},{33,49},{49,33},{2,18}... | collective-permute-start | bytes 6152 | tf_op jit(solution)/shard_map/ppermute | solution.py:469
  123.8 11.6 %collective-permute-start.1 = (f32[2,256]{1,0:T(2,128)S(1)}, f32[2,256]{1,0:T(2,128)S(1)}, u32[]{:S(2)}, u32[]{:S(2)}) collective-permute-start(f32[2,256]{1,0:T(2,128)S(1)} %reduce_sum.18), channel_id=1, source_target_pairs={{0,32},{16,48},{32,0},{48,16},{1,33},{17,49},{33,1},{49,17},{2,34}... | collective-permute-start | bytes 6152 | tf_op jit(solution)/shard_map/ppermute | solution.py:469
  135.3 2.1 %collective-permute-start.2 = (f32[2,256]{1,0:T(2,128)S(1)}, f32[2,256]{1,0:T(2,128)S(1)}, u32[]{:S(2)}, u32[]{:S(2)}) collective-permute-start(f32[2,256]{1,0:T(2,128)S(1)} %reduce_sum.18), channel_id=1, source_target_pairs={{0,48},{16,32},{32,16},{48,0},{1,49},{17,33},{33,17},{49,1},{2,50}... | collective-permute-start | bytes 6152 | tf_op jit(solution)/shard_map/ppermute | solution.py:469
  137.5 0.0 collective-permute-done
  137.5 8.9 %collective-permute-done.1 = f32[2,256]{1,0:T(2,128)S(1)} collective-permute-done((f32[2,256]{1,0:T(2,128)S(1)}, f32[2,256]{1,0:T(2,128)S(1)}, u32[]{:S(2)}, u32[]{:S(2)}) %collective-permute-start.1) | collective-permute-done | bytes 2080 | tf_op jit(solution)/shard_map/ppermute | solution.py:469
  146.4 2.0 %collective-permute-done.2 = f32[2,256]{1,0:T(2,128)S(1)} collective-permute-done((f32[2,256]{1,0:T(2,128)S(1)}, f32[2,256]{1,0:T(2,128)S(1)}, u32[]{:S(2)}, u32[]{:S(2)}) %collective-permute-start.2) | collective-permute-done | bytes 2080 | tf_op jit(solution)/shard_map/ppermute | solution.py:469
  148.4 0.6 slice_reduce_fusion
  149.0 0.1 reshape_squeeze.3
  149.1 0.6 reduce_sum.19
  149.7 0.0 all-to-all-done.2.in_ref
  149.7 0.0 copy-start
  149.7 1.2 copy-done
  150.9 2.7 %shard_map.114 = (bf16[128,4096]{1,0:T(8,128)(2,1)}, bf16[128,512]{1,0:T(8,128)(2,1)}) custom-call(bf16[16,384,128]{2,1,0:T(8,128)(2,1)} %copy-done), custom_call_target="tpu_custom_call" | custom-call | tf_op jit(solution)/shard_map/pallas_call | solution.py:472
  (2 shorter events, 0.0 us)
Async XLA Ops:
  65.5 39.1 %all-to-all-start.3 = ((f32[16,2,256]{2,1,0:T(2,128)}), f32[16,2,256]{2,1,0:T(2,128)S(1)}, u32[]{:S(2)}, u32[]{:S(2)}) async-start(f32[16,2,256]{2,1,0:T(2,128)} %shard_map.115), calls=%async_computation.3 | async-start | bytes 65536 | tf_op jit(solution)/shard_map/all_to_all | solution.py:382
  104.6 45.1 %all-to-all-start.2 = ((bf16[16,384,128]{2,1,0:T(8,128)(2,1)}), bf16[16,384,128]{2,1,0:T(8,128)(2,1)S(1)}, u32[]{:S(2)}, u32[]{:S(2)}) async-start(bf16[16,384,128]{2,1,0:T(8,128)(2,1)} %shard_map.113), calls=%async_computation.2 | async-start | bytes 3145728 | tf_op jit(solution)/shard_map/all_to_all | solution.py:382
  108.3 29.2 %collective-permute-start = (f32[2,256]{1,0:T(2,128)S(1)}, f32[2,256]{1,0:T(2,128)S(1)}, u32[]{:S(2)}, u32[]{:S(2)}) collective-permute-start(f32[2,256]{1,0:T(2,128)S(1)} %reduce_sum.18), channel_id=1, source_target_pairs={{0,16},{16,0},{32,48},{48,32},{1,17},{17,1},{33,49},{49,33},{2,18}... | collective-permute-start | bytes 6152 | tf_op jit(solution)/shard_map/ppermute | solution.py:469
  123.8 22.7 %collective-permute-start.1 = (f32[2,256]{1,0:T(2,128)S(1)}, f32[2,256]{1,0:T(2,128)S(1)}, u32[]{:S(2)}, u32[]{:S(2)}) collective-permute-start(f32[2,256]{1,0:T(2,128)S(1)} %reduce_sum.18), channel_id=1, source_target_pairs={{0,32},{16,48},{32,0},{48,16},{1,33},{17,49},{33,1},{49,17},{2,34}... | collective-permute-start | bytes 6152 | tf_op jit(solution)/shard_map/ppermute | solution.py:469
  135.3 13.0 %collective-permute-start.2 = (f32[2,256]{1,0:T(2,128)S(1)}, f32[2,256]{1,0:T(2,128)S(1)}, u32[]{:S(2)}, u32[]{:S(2)}) collective-permute-start(f32[2,256]{1,0:T(2,128)S(1)} %reduce_sum.18), channel_id=1, source_target_pairs={{0,48},{16,32},{32,16},{48,0},{1,49},{17,33},{33,17},{49,1},{2,50}... | collective-permute-start | bytes 6152 | tf_op jit(solution)/shard_map/ppermute | solution.py:469
  149.7 1.2 copy-start

commit v5 on v4

--- a/solution.py
+++ b/solution.py
@@ -25,6 +25,7 @@
 PACK_STEPS = 2
 GAIN_BLOCKS = 8
 FAR = -1e30
+HELD = 11
 X_AT, UP_AT, WRITE_AT, READ_AT, TAIL_AT, ROWS = 0, 256, 512, 640, 768, 784
 
 
@@ -60,44 +61,42 @@
     return jnp.concatenate([ref[b, at : at + T], ref[b, at + T : at + 2 * T]], axis=1).astype(F32)
 
 
-def rows_of(tail):
-    upto = (
-        lax.broadcasted_iota(jnp.int32, (T, T), 0) <= lax.broadcasted_iota(jnp.int32, (T, T), 1)
-    ).astype(F32).astype(BF16)
-    tail = tail.astype(F32)
-    step = tail[:8] / 16.0
-    high = pltpu.roll(tail[:8], HEADS, 0).astype(BF16)
-    whole = contract(high, upto, ((1,), (0,))) * 256.0 + contract(
-        tail[8:].astype(BF16), upto, ((1,), (0,))
-    )
-    log_decay = -(whole / 65536.0)
-    last = jnp.broadcast_to(log_decay[:, T - 1 : T], (8, T))
-    ending = jnp.exp(last - log_decay) * step
-    readout = jnp.exp(log_decay)
-    block_decay = jnp.exp(last).astype(BF16).astype(F32)
-    return log_decay, step, block_decay, ending, readout
-
-
-def scalars(tail):
-    log_decay, step, block_decay, ending, readout = rows_of(tail)
-    cols = jnp.transpose(jnp.concatenate([log_decay, step, ending, readout], axis=0))
-    return log_decay, step, block_decay, cols
-
-
 def thirds(rows):
     high = rows.astype(BF16).astype(F32)
     middle = (rows - high).astype(BF16).astype(F32)
     return high, middle, rows - high - middle
 
 
+def prepare(tail_ref, held):
+    upto = (
+        lax.broadcasted_iota(jnp.int32, (T, T), 0) <= lax.broadcasted_iota(jnp.int32, (T, T), 1)
+    ).astype(F32).astype(BF16)
+    tail = tail_ref[...].reshape(2 * T, T)
+    sums = contract(tail, upto, ((1,), (0,))).reshape(D, 2, 8, T)
+    step = tail.astype(F32).reshape(D, 2, 8, T)[:, 0].reshape(T, T) / 16.0
+    whole = pltpu.roll(sums[:, 0].reshape(T, T), T - HEADS, 0) * 256.0 + sums[:, 1].reshape(T, T)
+    log_decay = -(whole / 65536.0)
+    last = jnp.broadcast_to(log_decay[:, T - 1 : T], (T, T))
+    ending = jnp.exp(last - log_decay) * step
+    block_decay = jnp.exp(last).astype(BF16).astype(F32)
+    pieces = (*thirds(log_decay), *thirds(ending), *thirds(jnp.exp(log_decay)), step, block_decay)
+    for n, rows in enumerate(pieces):
+        held[n] = rows
+
+
+def kept(held, block):
+    rows = pl.ds(pl.multiple_of(8 * block, 8), 8)
+    got = [held[n, rows, :] for n in range(HELD)]
+    return got[:3], got[3:6], got[6:9], got[9], got[10]
+
+
 def head_marks(rows, width):
     row = lax.broadcasted_iota(jnp.int32, (rows, HEADS * width), 0) % 8
     lane = lax.broadcasted_iota(jnp.int32, (rows, HEADS * width), 1) // width
     return (row == lane).astype(F32)
 
 
-def gaps(log_decay, marks):
-    parts = thirds(log_decay)
+def gaps(parts, marks):
     place = lax.broadcasted_iota(jnp.int32, (8, T), 0)
     minus = []
     for j in range(HEADS):
@@ -110,26 +109,12 @@
     return contract(left, right, ((0,), (0,)))
 
 
-def spread_two(ending, readout, marks):
-    both = []
-    for rows in (ending, readout):
-        left = jnp.concatenate(thirds(rows), axis=0).astype(BF16)
-        both.append(contract(left, marks, ((0,), (0,))))
-    return both
+def spread(parts, marks):
+    return contract(jnp.concatenate(parts, axis=0).astype(BF16), marks, ((0,), (0,)))
 
 
 def low_half(shape):
     return lax.broadcasted_iota(jnp.int32, shape, len(shape) - 1) < P_SIZE
-
-
-def spread(cols, at):
-    mask = low_half((T, 128))
-    pairs = []
-    for i in range(HEADS // 2):
-        a = jnp.broadcast_to(cols[:, at + 2 * i : at + 2 * i + 1], (T, 128))
-        b = jnp.broadcast_to(cols[:, at + 2 * i + 1 : at + 2 * i + 2], (T, 128))
-        pairs.append(jnp.where(mask, a, b))
-    return jnp.concatenate(pairs, axis=1)
 
 
 def spread_rows(rows):
@@ -158,13 +143,16 @@
     )
 
 
-def forward_kernel(in_ref, gain_ref, skip_ref, mo_ref, carried_ref, stats_ref, carry, sums):
+def forward_kernel(
+    in_ref, tail_ref, gain_ref, skip_ref, mo_ref, carried_ref, stats_ref, carry, sums, held
+):
     step_id = pl.program_id(0)
 
     @pl.when(step_id == 0)
     def _():
         carry[...] = jnp.zeros_like(carry)
         sums[...] = jnp.zeros_like(sums)
+        prepare(tail_ref, held)
 
     gain = gain_ref[...]
     skip = skip_lanes(skip_ref)
@@ -181,9 +169,10 @@
         up = wide(in_ref, b, UP_AT)
         write = in_ref[b, WRITE_AT : WRITE_AT + T]
         read = in_ref[b, READ_AT : READ_AT + T]
-        log_decay, step, block_decay, ending, readout = rows_of(in_ref[b, TAIL_AT:])
-        gap = gaps(log_decay, wide_marks)
-        ending, readout = spread_two(ending, readout, marks)
+        at = BLOCKS_PER_STEP * step_id + b
+        decays, ending, readout, step, block_decay = kept(held, at)
+        gap = gaps(decays, wide_marks)
+        ending, readout = spread(ending, marks), spread(readout, marks)
         scores = contract(read, write, ((1,), (1,)))
         inner = []
         for i in range(HEADS // 2):
@@ -209,7 +198,6 @@
         )
         square = jnp.sum(out * out, axis=1, keepdims=True)
         cross = jnp.sum(up * gain * out, axis=1, keepdims=True)
-        at = BLOCKS_PER_STEP * step_id + b
         found = jnp.where(lane_id == at, square, jnp.where(lane_id == D + at, cross, found))
         results.append((out, carried))
     for b, (out, carried) in enumerate(results):
@@ -277,7 +265,17 @@
 
 
 def backward_kernel(
-    in_ref, mo_ref, carried_ref, stats_ref, gain_ref, skip_ref, out_ref, carry, sums
+    in_ref,
+    tail_ref,
+    mo_ref,
+    carried_ref,
+    stats_ref,
+    gain_ref,
+    skip_ref,
+    out_ref,
+    carry,
+    sums,
+    held,
 ):
     step_id = pl.program_id(0)
 
@@ -285,12 +283,16 @@
     def _():
         carry[...] = jnp.zeros_like(carry)
         shared_sums(stats_ref, sums)
+        prepare(tail_ref, held)
 
     gain = gain_ref[...]
     skip = skip_lanes(skip_ref)
     row_id = lax.broadcasted_iota(jnp.int32, (T, T), 0)
     lane_id = lax.broadcasted_iota(jnp.int32, (T, T), 1)
     later = row_id <= lane_id
+    marks = head_marks(24, P_SIZE).astype(BF16)
+    wide_marks = head_marks(24, T)
+    step_marks = head_marks(8, T).astype(BF16)
     state = carry[...]
     results = []
     first = BLOCKS_PER_STEP * (STEPS - 1 - step_id)
@@ -300,9 +302,12 @@
         write = in_ref[b, WRITE_AT : WRITE_AT + T]
         read = in_ref[b, READ_AT : READ_AT + T]
         out = mo_ref[b]
-        log_decay, _, block_decay, cols = scalars(in_ref[b, TAIL_AT:])
+        decays, ending, readout, step, block_decay = kept(held, first + b)
+        gap = gaps(decays, wide_marks)
+        ending, readout = spread(ending, marks), spread(readout, marks)
+        step = spread([step], step_marks)
         _, delta = normalise(sums, first + b, out, up, gain)
-        scaled = (delta * spread(cols, 24)).astype(BF16)
+        scaled = (delta * readout).astype(BF16)
         half = delta.astype(BF16)
         scores = contract(write, read, ((1,), (1,)))
         score_grad = jnp.zeros((T, T), F32)
@@ -312,8 +317,8 @@
             mix_grad = contract(two_heads(x[:, pair]), half[:, pair], ((1,), (1,)))
             mixing = []
             for n, j in enumerate((2 * i, 2 * i + 1)):
-                gap = jnp.where(later, log_decay[j : j + 1] - cols[:, j : j + 1], FAR)
-                weight = jnp.exp(gap) * cols[:, 8 + j : 9 + j]
+                lanes = slice(T * j, T * (j + 1))
+                weight = jnp.exp(jnp.where(later, -gap[:, lanes], FAR)) * step[:, lanes]
                 mixing.append((scores * weight).astype(BF16))
                 score_grad = score_grad + weight * mix_grad[T * n : T * (n + 1)]
             mixed.append(
@@ -324,7 +329,7 @@
         carried_grad = state.astype(BF16)
         mixer_grad = (
             jnp.concatenate(mixed, axis=1)
-            + spread(cols, 16) * contract(write, carried_grad, ((1,), (0,)))
+            + ending * contract(write, carried_grad, ((1,), (0,)))
             + skip * delta
         )
         read_grad = contract(score_grad.astype(BF16), write, ((0,), (0,))) + contract(
@@ -356,6 +361,7 @@
     return pl.BlockSpec(shape, lambda i: (0,) * len(shape))
 
 
+TAILS = pl.BlockSpec((D, ROWS - TAIL_AT, 128), lambda i: (0, TAIL_AT // (ROWS - TAIL_AT), 0))
 SCALARS = pl.BlockSpec(memory_space=pltpu.SMEM)
 
 
@@ -412,7 +418,7 @@
         mixer_out, carried, stats = call(
             forward_kernel,
             STEPS,
-            [pl.BlockSpec((size, ROWS, 128), along), whole((1, LANES)), SCALARS],
+            [pl.BlockSpec((size, TAIL_AT, 128), along), TAILS, whole((1, LANES)), SCALARS],
             [
                 pl.BlockSpec((size, T, LANES), along),
                 pl.BlockSpec((size, N, LANES), along),
@@ -423,9 +429,13 @@
                 shape((D, N, LANES), BF16),
                 shape((4, 2 * D, T), F32),
             ],
-            [pltpu.VMEM((N, LANES), F32), pltpu.VMEM((T, T), F32)],
+            [
+                pltpu.VMEM((N, LANES), F32),
+                pltpu.VMEM((T, T), F32),
+                pltpu.VMEM((HELD, T, T), F32),
+            ],
             interpret=interpret,
-        )(blocks, gain, skip_gain)
+        )(blocks, blocks, gain, skip_gain)
         stats = exchange(stats, "seq_1")
 
         near = lax.axis_size(NEAR)
@@ -449,7 +459,8 @@
             backward_kernel,
             STEPS,
             [
-                pl.BlockSpec((size, ROWS, 128), back),
+                pl.BlockSpec((size, TAIL_AT, 128), back),
+                TAILS,
                 pl.BlockSpec((size, T, LANES), back),
                 pl.BlockSpec((size, N, LANES), back),
                 whole((4, 2 * D, T)),
@@ -458,10 +469,14 @@
             ],
             pl.BlockSpec((size, 3 * T, 128), back),
             shape((D, 3 * T, 128), BF16),
-            [pltpu.VMEM((N, LANES), F32), pltpu.VMEM((6, D, T), F32)],
+            [
+                pltpu.VMEM((N, LANES), F32),
+                pltpu.VMEM((6, D, T), F32),
+                pltpu.VMEM((HELD, T, T), F32),
+            ],
             flops=1 << 34,
             interpret=interpret,
-        )(blocks, mixer_out, carried, stats, gain, skip_gain)
+        )(blocks, blocks, mixer_out, carried, stats, gain, skip_gain)
         grads = exchange(grads, SEQ)
         parts = jnp.sum(parts, axis=0)
         if lax.axis_size("z_high") == 4:

time: 155 us -> 149 us (0.961)
  Pallas kernels: 35.5 us -> 29.6 us
    pallas_call x2, Pallas kernels: 26.2 us -> 20.3 us  [the longest x1 12 us: mixer(): call(backward_kernel, STEPS, [pl.BlockSpec((size, TAIL_AT, 128), back), T...]
  transfers between devices with their start and end apart: 5 -> 5, of which waited for: 2 -> 2; matrix products, arithmetic and copies ran while one was open for 1% -> 1% of each run, Pallas kernels for 10% -> 8%
where the time goes in v5:
time: 149 us; the launch traced here: 148 us
  starting transfers between devices  57.3 us (38%)
  blocking collectives  46.7 us (31%)
  Pallas kernels  29.6 us (20%)
  waiting for transfers between devices  10.9 us (7%)
  local copies, waits for them, and re-layouts  1.82 us (1%)
    all_to_all x2, blocking collectives, exchange(): return lax.all_to_all(array, axes, split_axis=0, concat_axis=0, tiled=True)  46.7 us
    ppermute x3, starting transfers between devices, mixer(): lax.ppermute(parts, 'z_high', [(i, i ^ d) for i in range(4)])  29.2 us
    all_to_all x2, starting transfers between devices, exchange(): return lax.all_to_all(array, axes, split_axis=0, concat_axis=0, tiled=True)  28.1 us
    pallas_call x1, Pallas kernels, mixer(): call(backward_kernel, STEPS, [pl.BlockSpec((size, TAIL_AT, 128), back), T...  12 us
    ppermute x3, waiting for transfers between devices, mixer(): lax.ppermute(parts, 'z_high', [(i, i ^ d) for i in range(4)])  10.9 us
    pallas_call x1, Pallas kernels, mixer(): call(forward_kernel, STEPS, [pl.BlockSpec((size, TAIL_AT, 128), along), T...  8.31 us
    pallas_call x1, Pallas kernels, mixer(): call(gain_kernel, D // GAIN_BLOCKS, [pl.BlockSpec((GAIN_BLOCKS, WRITE_AT,...  3.42 us
    pallas_call x1, Pallas kernels, mixer(): call(pack_kernel, PACK_STEPS, [pl.BlockSpec((T, H * P_SIZE // PACK_STEPS)...  3.2 us
  transfers between devices with their start and end apart: 5, of which 2 were waited for; matrix products, arithmetic and copies ran while one was open for 1% of the time, Pallas kernels for 8%

profile of v5, /device:TPU:1, one launch (start us, length us, event | category | flops | bytes accessed | tf_op | source)
XLA Modules:
  0.0 147.6 jit_solution(6354856256993705545)
XLA Ops:
  0.6 3.2 %shard_map.111 = bf16[16,784,128]{2,1,0:T(8,128)(2,1)} custom-call(bf16[128,4096]{1,0:T(8,128)(2,1)} %bitcast.14, bf16[128,4096]{1,0:T(8,128)(2,1)} %bitcast.15, bf16[128,512]{1,0:T(8,128)(2,1)} %bitcast.16, bf16[128,512]{1,0:T(8,128)(2,1)} %bitcast.17, s32[64,128]{1,0:T(8,128)} %bitcast.18, s32[64,128]{1,0:T(8,128)} %bitcast.19), custom_call_target="tpu_custom_call" | custom-call | bytes 1048576 | tf_op jit(solution)/shard_map/pallas_call | solution.py:392
  3.8 38.3 %all_to_all.20.in_ref.tail_ref = bf16[16,784,128]{2,1,0:T(8,128)(2,1)} all-to-all(bf16[16,784,128]{2,1,0:T(8,128)(2,1)} %shard_map.111), channel_id=1, replica_groups=mesh['seq_0'=4,'seq_1'=4,'z_high'=4,'z_low'=8,'core'=2] {'seq_0','seq_1'}, dimensions={0} | all-to-all | bytes 6422528 | tf_op jit(solution)/shard_map/all_to_all | solution.py:388
  42.1 8.3 %shard_map.112 = (f32[16,128,256]{2,1,0:T(8,128)}, bf16[16,128,256]{2,1,0:T(8,128)(2,1)}, f32[4,32,128]{2,1,0:T(8,128)}) custom-call(bf16[16,784,128]{2,1,0:T(8,128)(2,1)} %all_to_all.20.in_ref.tail_ref, bf16[16,784,128]{2,1,0:T(8,128)(2,1)} %all_to_all.20.in_ref.tail_ref, f32[1,256]{1,0:T(1,128)} %bitcast.20, f32[4]{0:T(128)} %skip_ref.3), custom_call_target="tpu_custom_call" | custom-call | bytes 1048576 | tf_op jit(solution)/shard_map/pallas_call | solution.py:418
  50.4 8.4 %all_to_all.21.stats_ref = f32[4,32,128]{2,1,0:T(8,128)} all-to-all(f32[4,32,128]{2,1,0:T(8,128)} %get-tuple-element.11), channel_id=1, replica_groups=mesh['seq_0'=4,'seq_1'=4,'z_high'=4,'z_low'=8,'core'=2] {'seq_1'}, dimensions={0} | all-to-all | bytes 131072 | tf_op jit(solution)/shard_map/all_to_all | solution.py:388
  58.9 3.4 %shard_map.115 = f32[16,2,256]{2,1,0:T(2,128)} custom-call(bf16[16,784,128]{2,1,0:T(8,128)(2,1)} %all_to_all.20.in_ref.tail_ref, f32[16,128,256]{2,1,0:T(8,128)} %get-tuple-element.9.mo_ref, f32[4,32,128]{2,1,0:T(8,128)} %all_to_all.21.stats_ref, f32[1,256]{1,0:T(1,128)} %bitcast.21), custom_call_target="tpu_custom_call" | custom-call | bytes 1048576 | tf_op jit(solution)/shard_map/pallas_call | solution.py:442
  62.3 24.4 %all-to-all-start.3 = ((f32[16,2,256]{2,1,0:T(2,128)}), f32[16,2,256]{2,1,0:T(2,128)S(1)}, u32[]{:S(2)}, u32[]{:S(2)}) async-start(f32[16,2,256]{2,1,0:T(2,128)} %shard_map.115), calls=%async_computation.3 | async-start | bytes 65536 | tf_op jit(solution)/shard_map/all_to_all | solution.py:388
  86.7 12.0 %shard_map.113 = bf16[16,384,128]{2,1,0:T(8,128)(2,1)} custom-call(bf16[16,784,128]{2,1,0:T(8,128)(2,1)} %all_to_all.20.in_ref.tail_ref, bf16[16,784,128]{2,1,0:T(8,128)(2,1)} %all_to_all.20.in_ref.tail_ref, f32[16,128,256]{2,1,0:T(8,128)} %get-tuple-element.9.mo_ref, bf16[16,128,256]{2,1,0:T(8,128)(2,1)} %get-tuple-element.10.carried_ref, ...), custom_call_target="tpu_custom_call" | custom-call | flops 17179869184 | bytes 1048576 | tf_op jit(solution)/shard_map/pallas_call | solution.py:458
  98.6 0.0 all-to-all-done.3
  98.6 3.7 %all-to-all-start.2 = ((bf16[16,384,128]{2,1,0:T(8,128)(2,1)}), bf16[16,384,128]{2,1,0:T(8,128)(2,1)S(1)}, u32[]{:S(2)}, u32[]{:S(2)}) async-start(bf16[16,384,128]{2,1,0:T(8,128)(2,1)} %shard_map.113), calls=%async_computation.2 | async-start | bytes 3145728 | tf_op jit(solution)/shard_map/all_to_all | solution.py:388
  102.4 15.4 %collective-permute-start = (f32[2,256]{1,0:T(2,128)S(1)}, f32[2,256]{1,0:T(2,128)S(1)}, u32[]{:S(2)}, u32[]{:S(2)}) collective-permute-start(f32[2,256]{1,0:T(2,128)S(1)} %reduce_sum.18), channel_id=1, source_target_pairs={{0,16},{16,0},{32,48},{48,32},{1,17},{17,1},{33,49},{49,33},{2,18}... | collective-permute-start | bytes 6152 | tf_op jit(solution)/shard_map/ppermute | solution.py:484
  117.8 11.6 %collective-permute-start.1 = (f32[2,256]{1,0:T(2,128)S(1)}, f32[2,256]{1,0:T(2,128)S(1)}, u32[]{:S(2)}, u32[]{:S(2)}) collective-permute-start(f32[2,256]{1,0:T(2,128)S(1)} %reduce_sum.18), channel_id=1, source_target_pairs={{0,32},{16,48},{32,0},{48,16},{1,33},{17,49},{33,1},{49,17},{2,34}... | collective-permute-start | bytes 6152 | tf_op jit(solution)/shard_map/ppermute | solution.py:484
  129.4 2.1 %collective-permute-start.2 = (f32[2,256]{1,0:T(2,128)S(1)}, f32[2,256]{1,0:T(2,128)S(1)}, u32[]{:S(2)}, u32[]{:S(2)}) collective-permute-start(f32[2,256]{1,0:T(2,128)S(1)} %reduce_sum.18), channel_id=1, source_target_pairs={{0,48},{16,32},{32,16},{48,0},{1,49},{17,33},{33,17},{49,1},{2,50}... | collective-permute-start | bytes 6152 | tf_op jit(solution)/shard_map/ppermute | solution.py:484
  131.6 0.0 collective-permute-done
  131.6 8.9 %collective-permute-done.1 = f32[2,256]{1,0:T(2,128)S(1)} collective-permute-done((f32[2,256]{1,0:T(2,128)S(1)}, f32[2,256]{1,0:T(2,128)S(1)}, u32[]{:S(2)}, u32[]{:S(2)}) %collective-permute-start.1) | collective-permute-done | bytes 2080 | tf_op jit(solution)/shard_map/ppermute | solution.py:484
  140.5 2.0 %collective-permute-done.2 = f32[2,256]{1,0:T(2,128)S(1)} collective-permute-done((f32[2,256]{1,0:T(2,128)S(1)}, f32[2,256]{1,0:T(2,128)S(1)}, u32[]{:S(2)}, u32[]{:S(2)}) %collective-permute-start.2) | collective-permute-done | bytes 2080 | tf_op jit(solution)/shard_map/ppermute | solution.py:484
  142.5 0.6 slice_reduce_fusion
  143.0 0.1 reshape_squeeze.3
  143.1 0.6 reduce_sum.19
  143.8 0.0 all-to-all-done.2.in_ref
  143.8 0.0 copy-start
  143.8 1.2 copy-done
  144.9 2.7 %shard_map.114 = (bf16[128,4096]{1,0:T(8,128)(2,1)}, bf16[128,512]{1,0:T(8,128)(2,1)}) custom-call(bf16[16,384,128]{2,1,0:T(8,128)(2,1)} %copy-done), custom_call_target="tpu_custom_call" | custom-call | tf_op jit(solution)/shard_map/pallas_call | solution.py:487
  (2 shorter events, 0.0 us)
Async XLA Ops:
  62.3 36.4 %all-to-all-start.3 = ((f32[16,2,256]{2,1,0:T(2,128)}), f32[16,2,256]{2,1,0:T(2,128)S(1)}, u32[]{:S(2)}, u32[]{:S(2)}) async-start(f32[16,2,256]{2,1,0:T(2,128)} %shard_map.115), calls=%async_computation.3 | async-start | bytes 65536 | tf_op jit(solution)/shard_map/all_to_all | solution.py:388
  98.6 45.1 %all-to-all-start.2 = ((bf16[16,384,128]{2,1,0:T(8,128)(2,1)}), bf16[16,384,128]{2,1,0:T(8,128)(2,1)S(1)}, u32[]{:S(2)}, u32[]{:S(2)}) async-start(bf16[16,384,128]{2,1,0:T(8,128)(2,1)} %shard_map.113), calls=%async_computation.2 | async-start | bytes 3145728 | tf_op jit(solution)/shard_map/all_to_all | solution.py:388
  102.4 29.2 %collective-permute-start = (f32[2,256]{1,0:T(2,128)S(1)}, f32[2,256]{1,0:T(2,128)S(1)}, u32[]{:S(2)}, u32[]{:S(2)}) collective-permute-start(f32[2,256]{1,0:T(2,128)S(1)} %reduce_sum.18), channel_id=1, source_target_pairs={{0,16},{16,0},{32,48},{48,32},{1,17},{17,1},{33,49},{49,33},{2,18}... | collective-permute-start | bytes 6152 | tf_op jit(solution)/shard_map/ppermute | solution.py:484
  117.8 22.7 %collective-permute-start.1 = (f32[2,256]{1,0:T(2,128)S(1)}, f32[2,256]{1,0:T(2,128)S(1)}, u32[]{:S(2)}, u32[]{:S(2)}) collective-permute-start(f32[2,256]{1,0:T(2,128)S(1)} %reduce_sum.18), channel_id=1, source_target_pairs={{0,32},{16,48},{32,0},{48,16},{1,33},{17,49},{33,1},{49,17},{2,34}... | collective-permute-start | bytes 6152 | tf_op jit(solution)/shard_map/ppermute | solution.py:484
  129.4 13.0 %collective-permute-start.2 = (f32[2,256]{1,0:T(2,128)S(1)}, f32[2,256]{1,0:T(2,128)S(1)}, u32[]{:S(2)}, u32[]{:S(2)}) collective-permute-start(f32[2,256]{1,0:T(2,128)S(1)} %reduce_sum.18), channel_id=1, source_target_pairs={{0,48},{16,32},{32,16},{48,0},{1,49},{17,33},{33,17},{49,1},{2,50}... | collective-permute-start | bytes 6152 | tf_op jit(solution)/shard_map/ppermute | solution.py:484
  143.8 1.2 copy-start

commit v6 on v5

--- a/solution.py
+++ b/solution.py
@@ -347,7 +347,7 @@
 
 
 def unpack_kernel(in_ref, mixer_ref, read_ref):
-    for g in range(G):
+    for g in range(G // 2):
         total = jnp.zeros((T, N), F32)
         for d in range(4 * g, 4 * g + 4):
             for half in range(2):
@@ -480,12 +480,15 @@
         grads = exchange(grads, SEQ)
         parts = jnp.sum(parts, axis=0)
         if lax.axis_size("z_high") == 4:
-            one, two, three = (
-                lax.ppermute(parts, "z_high", [(i, i ^ d) for i in range(4)]) for d in (1, 2, 3)
+            two, one, three = (
+                lax.ppermute(parts, "z_high", [(i, i ^ d) for i in range(4)]) for d in (2, 1, 3)
             )
             parts = (parts + one) + (two + three)
         mixer_grad, read_grad = pl.pallas_call(
             unpack_kernel,
+            grid=(2,),
+            in_specs=[pl.BlockSpec((D // 2, 3 * T, 128), along)],
+            out_specs=[pl.BlockSpec((T, H * P_SIZE // 2), column), pl.BlockSpec((T, G * N // 2), column)],
             out_shape=[shape((T, H * P_SIZE), BF16), shape((T, G * N), BF16)],
             interpret=interpret,
         )(grads)

time: 149 us -> 148 us (level)
  no operation moved by 1% of the time
where the time goes in v6:
time: 148 us; the launch traced here: 147 us
  starting transfers between devices  57.3 us (39%)
  blocking collectives  46.7 us (32%)
  Pallas kernels  29.2 us (20%)
  waiting for transfers between devices  10.9 us (7%)
  local copies, waits for them, and re-layouts  1.82 us (1%)
    all_to_all x2, blocking collectives, exchange(): return lax.all_to_all(array, axes, split_axis=0, concat_axis=0, tiled=True)  46.7 us
    ppermute x3, starting transfers between devices, mixer(): lax.ppermute(parts, 'z_high', [(i, i ^ d) for i in range(4)])  29.2 us
    all_to_all x2, starting transfers between devices, exchange(): return lax.all_to_all(array, axes, split_axis=0, concat_axis=0, tiled=True)  28.1 us
    pallas_call x1, Pallas kernels, mixer(): call(backward_kernel, STEPS, [pl.BlockSpec((size, TAIL_AT, 128), back), T...  12 us
    ppermute x3, waiting for transfers between devices, mixer(): lax.ppermute(parts, 'z_high', [(i, i ^ d) for i in range(4)])  10.9 us
    pallas_call x1, Pallas kernels, mixer(): call(forward_kernel, STEPS, [pl.BlockSpec((size, TAIL_AT, 128), along), T...  8.31 us
    pallas_call x1, Pallas kernels, mixer(): call(gain_kernel, D // GAIN_BLOCKS, [pl.BlockSpec((GAIN_BLOCKS, WRITE_AT,...  3.42 us
    pallas_call x1, Pallas kernels, mixer(): call(pack_kernel, PACK_STEPS, [pl.BlockSpec((T, H * P_SIZE // PACK_STEPS)...  3.2 us
  transfers between devices with their start and end apart: 5, of which 2 were waited for; matrix products, arithmetic and copies ran while one was open for 1% of the time, Pallas kernels for 8%

profile of v6, /device:TPU:1, one launch (start us, length us, event | category | flops | bytes accessed | tf_op | source)
XLA Modules:
  0.0 147.3 jit_solution(7461041255964184967)
XLA Ops:
  0.6 3.2 %shard_map.111 = bf16[16,784,128]{2,1,0:T(8,128)(2,1)} custom-call(bf16[128,4096]{1,0:T(8,128)(2,1)} %bitcast.14, bf16[128,4096]{1,0:T(8,128)(2,1)} %bitcast.15, bf16[128,512]{1,0:T(8,128)(2,1)} %bitcast.16, bf16[128,512]{1,0:T(8,128)(2,1)} %bitcast.17, s32[64,128]{1,0:T(8,128)} %bitcast.18, s32[64,128]{1,0:T(8,128)} %bitcast.19), custom_call_target="tpu_custom_call" | custom-call | bytes 1048576 | tf_op jit(solution)/shard_map/pallas_call | solution.py:392
  3.8 38.3 %all_to_all.20.in_ref.tail_ref = bf16[16,784,128]{2,1,0:T(8,128)(2,1)} all-to-all(bf16[16,784,128]{2,1,0:T(8,128)(2,1)} %shard_map.111), channel_id=1, replica_groups=mesh['seq_0'=4,'seq_1'=4,'z_high'=4,'z_low'=8,'core'=2] {'seq_0','seq_1'}, dimensions={0} | all-to-all | bytes 6422528 | tf_op jit(solution)/shard_map/all_to_all | solution.py:388
  42.1 8.3 %shard_map.112 = (f32[16,128,256]{2,1,0:T(8,128)}, bf16[16,128,256]{2,1,0:T(8,128)(2,1)}, f32[4,32,128]{2,1,0:T(8,128)}) custom-call(bf16[16,784,128]{2,1,0:T(8,128)(2,1)} %all_to_all.20.in_ref.tail_ref, bf16[16,784,128]{2,1,0:T(8,128)(2,1)} %all_to_all.20.in_ref.tail_ref, f32[1,256]{1,0:T(1,128)} %bitcast.20, f32[4]{0:T(128)} %skip_ref.3), custom_call_target="tpu_custom_call" | custom-call | bytes 1048576 | tf_op jit(solution)/shard_map/pallas_call | solution.py:418
  50.4 8.4 %all_to_all.21.stats_ref = f32[4,32,128]{2,1,0:T(8,128)} all-to-all(f32[4,32,128]{2,1,0:T(8,128)} %get-tuple-element.11), channel_id=1, replica_groups=mesh['seq_0'=4,'seq_1'=4,'z_high'=4,'z_low'=8,'core'=2] {'seq_1'}, dimensions={0} | all-to-all | bytes 131072 | tf_op jit(solution)/shard_map/all_to_all | solution.py:388
  58.9 3.4 %shard_map.115 = f32[16,2,256]{2,1,0:T(2,128)} custom-call(bf16[16,784,128]{2,1,0:T(8,128)(2,1)} %all_to_all.20.in_ref.tail_ref, f32[16,128,256]{2,1,0:T(8,128)} %get-tuple-element.9.mo_ref, f32[4,32,128]{2,1,0:T(8,128)} %all_to_all.21.stats_ref, f32[1,256]{1,0:T(1,128)} %bitcast.21), custom_call_target="tpu_custom_call" | custom-call | bytes 1048576 | tf_op jit(solution)/shard_map/pallas_call | solution.py:442
  62.3 24.4 %all-to-all-start.3 = ((f32[16,2,256]{2,1,0:T(2,128)}), f32[16,2,256]{2,1,0:T(2,128)S(1)}, u32[]{:S(2)}, u32[]{:S(2)}) async-start(f32[16,2,256]{2,1,0:T(2,128)} %shard_map.115), calls=%async_computation.3 | async-start | bytes 65536 | tf_op jit(solution)/shard_map/all_to_all | solution.py:388
  86.7 12.0 %shard_map.113 = bf16[16,384,128]{2,1,0:T(8,128)(2,1)} custom-call(bf16[16,784,128]{2,1,0:T(8,128)(2,1)} %all_to_all.20.in_ref.tail_ref, bf16[16,784,128]{2,1,0:T(8,128)(2,1)} %all_to_all.20.in_ref.tail_ref, f32[16,128,256]{2,1,0:T(8,128)} %get-tuple-element.9.mo_ref, bf16[16,128,256]{2,1,0:T(8,128)(2,1)} %get-tuple-element.10.carried_ref, ...), custom_call_target="tpu_custom_call" | custom-call | flops 17179869184 | bytes 1048576 | tf_op jit(solution)/shard_map/pallas_call | solution.py:458
  98.6 0.0 all-to-all-done.3
  98.6 3.7 %all-to-all-start.2 = ((bf16[16,384,128]{2,1,0:T(8,128)(2,1)}), bf16[16,384,128]{2,1,0:T(8,128)(2,1)S(1)}, u32[]{:S(2)}, u32[]{:S(2)}) async-start(bf16[16,384,128]{2,1,0:T(8,128)(2,1)} %shard_map.113), calls=%async_computation.2 | async-start | bytes 3145728 | tf_op jit(solution)/shard_map/all_to_all | solution.py:388
  102.4 15.4 %collective-permute-start = (f32[2,256]{1,0:T(2,128)S(1)}, f32[2,256]{1,0:T(2,128)S(1)}, u32[]{:S(2)}, u32[]{:S(2)}) collective-permute-start(f32[2,256]{1,0:T(2,128)S(1)} %reduce_sum.18), channel_id=1, source_target_pairs={{0,16},{16,0},{32,48},{48,32},{1,17},{17,1},{33,49},{49,33},{2,18}... | collective-permute-start | bytes 6152 | tf_op jit(solution)/shard_map/ppermute | solution.py:484
  117.8 11.6 %collective-permute-start.1 = (f32[2,256]{1,0:T(2,128)S(1)}, f32[2,256]{1,0:T(2,128)S(1)}, u32[]{:S(2)}, u32[]{:S(2)}) collective-permute-start(f32[2,256]{1,0:T(2,128)S(1)} %reduce_sum.18), channel_id=1, source_target_pairs={{0,32},{16,48},{32,0},{48,16},{1,33},{17,49},{33,1},{49,17},{2,34}... | collective-permute-start | bytes 6152 | tf_op jit(solution)/shard_map/ppermute | solution.py:484
  129.4 2.1 %collective-permute-start.2 = (f32[2,256]{1,0:T(2,128)S(1)}, f32[2,256]{1,0:T(2,128)S(1)}, u32[]{:S(2)}, u32[]{:S(2)}) collective-permute-start(f32[2,256]{1,0:T(2,128)S(1)} %reduce_sum.18), channel_id=1, source_target_pairs={{0,48},{16,32},{32,16},{48,0},{1,49},{17,33},{33,17},{49,1},{2,50}... | collective-permute-start | bytes 6152 | tf_op jit(solution)/shard_map/ppermute | solution.py:484
  131.6 0.0 collective-permute-done
  131.6 8.9 %collective-permute-done.1 = f32[2,256]{1,0:T(2,128)S(1)} collective-permute-done((f32[2,256]{1,0:T(2,128)S(1)}, f32[2,256]{1,0:T(2,128)S(1)}, u32[]{:S(2)}, u32[]{:S(2)}) %collective-permute-start.1) | collective-permute-done | bytes 2080 | tf_op jit(solution)/shard_map/ppermute | solution.py:484
  140.5 2.0 %collective-permute-done.2 = f32[2,256]{1,0:T(2,128)S(1)} collective-permute-done((f32[2,256]{1,0:T(2,128)S(1)}, f32[2,256]{1,0:T(2,128)S(1)}, u32[]{:S(2)}, u32[]{:S(2)}) %collective-permute-start.2) | collective-permute-done | bytes 2080 | tf_op jit(solution)/shard_map/ppermute | solution.py:484
  142.5 0.6 slice_reduce_fusion
  143.0 0.1 reshape_squeeze.3
  143.1 0.6 reduce_sum.19
  143.8 0.0 all-to-all-done.2.in_ref
  143.8 0.0 copy-start
  143.8 1.2 copy-done
  144.9 2.3 %shard_map.114 = (bf16[128,4096]{1,0:T(8,128)(2,1)}, bf16[128,512]{1,0:T(8,128)(2,1)}) custom-call(bf16[16,384,128]{2,1,0:T(8,128)(2,1)} %copy-done), custom_call_target="tpu_custom_call" | custom-call | tf_op jit(solution)/shard_map/pallas_call | solution.py:487
  (2 shorter events, 0.0 us)
Async XLA Ops:
  62.3 36.4 %all-to-all-start.3 = ((f32[16,2,256]{2,1,0:T(2,128)}), f32[16,2,256]{2,1,0:T(2,128)S(1)}, u32[]{:S(2)}, u32[]{:S(2)}) async-start(f32[16,2,256]{2,1,0:T(2,128)} %shard_map.115), calls=%async_computation.3 | async-start | bytes 65536 | tf_op jit(solution)/shard_map/all_to_all | solution.py:388
  98.6 45.1 %all-to-all-start.2 = ((bf16[16,384,128]{2,1,0:T(8,128)(2,1)}), bf16[16,384,128]{2,1,0:T(8,128)(2,1)S(1)}, u32[]{:S(2)}, u32[]{:S(2)}) async-start(bf16[16,384,128]{2,1,0:T(8,128)(2,1)} %shard_map.113), calls=%async_computation.2 | async-start | bytes 3145728 | tf_op jit(solution)/shard_map/all_to_all | solution.py:388
  102.4 29.2 %collective-permute-start = (f32[2,256]{1,0:T(2,128)S(1)}, f32[2,256]{1,0:T(2,128)S(1)}, u32[]{:S(2)}, u32[]{:S(2)}) collective-permute-start(f32[2,256]{1,0:T(2,128)S(1)} %reduce_sum.18), channel_id=1, source_target_pairs={{0,16},{16,0},{32,48},{48,32},{1,17},{17,1},{33,49},{49,33},{2,18}... | collective-permute-start | bytes 6152 | tf_op jit(solution)/shard_map/ppermute | solution.py:484
  117.8 22.7 %collective-permute-start.1 = (f32[2,256]{1,0:T(2,128)S(1)}, f32[2,256]{1,0:T(2,128)S(1)}, u32[]{:S(2)}, u32[]{:S(2)}) collective-permute-start(f32[2,256]{1,0:T(2,128)S(1)} %reduce_sum.18), channel_id=1, source_target_pairs={{0,32},{16,48},{32,0},{48,16},{1,33},{17,49},{33,1},{49,17},{2,34}... | collective-permute-start | bytes 6152 | tf_op jit(solution)/shard_map/ppermute | solution.py:484
  129.4 13.0 %collective-permute-start.2 = (f32[2,256]{1,0:T(2,128)S(1)}, f32[2,256]{1,0:T(2,128)S(1)}, u32[]{:S(2)}, u32[]{:S(2)}) collective-permute-start(f32[2,256]{1,0:T(2,128)S(1)} %reduce_sum.18), channel_id=1, source_target_pairs={{0,48},{16,32},{32,16},{48,0},{1,49},{17,33},{33,17},{49,1},{2,50}... | collective-permute-start | bytes 6152 | tf_op jit(solution)/shard_map/ppermute | solution.py:484
  143.8 1.2 copy-start
